TPU v7x, 16 devices: a 4x2x1 block of a 4x4x8 slice. The times are simulated.
16 devices in a mesh: dp: 2 (over y, z), tp: 8 (over x, core).
Axes of the slice: x: 4, y: 2, z: 1, core: 2. Of those that a mesh axis runs over, the one named last changes fastest.
The devices are a block of a 4x4x8 slice.
Arguments:
- ids: int32 [32, 256], P('dp'), parts along dimension 0
- E: bfloat16 [16384, 3072], P('tp')
- g: bfloat16 [3072], replicated
- W: bfloat16 [3072, 12288], P(None, 'tp')
- du: bfloat16 [32, 256, 12288], P('dp', None, 'tp'), parts along dimension 0
- dres: bfloat16 [32, 256, 3072], P('dp', 'tp'), parts along dimension 0
Outputs:
- output 1: bfloat16 [32, 256, 12288], P('dp', None, 'tp'), parts along dimension 0
- output 2: bfloat16 [32, 256, 3072], P('dp', 'tp'), parts along dimension 0
- output 3: float32 [32768, 3072], P(('dp', 'tp')), parts along dimension 0
- output 4: float32 [6144, 12288], P('dp', 'tp'), parts along dimension 0
- output 5: float32 [6144], P('dp'), parts along dimension 0
There are 2 independent parts. A program takes and returns all parts, laid end to end along the dimension named above; an argument that names none is the same for every part.
All inputs are finite; a program needn't handle non-finite values.
Results may differ from a plain program's by a relative error of at most 0.001.
Values are sent between devices in bfloat16 or wider.
A program may use at most 768 MiB of HBM per device.

v0:
```python
import jax
import jax.numpy as jnp
from jax import lax
from jax.sharding import PartitionSpec as P


EPS = 1e-6
ROWS = 176
CAP = 96
LANES = 128


def solution(mesh):
    ntp = mesh.shape["tp"]
    nch = ntp // 2
    f32, bf16, i32 = jnp.float32, jnp.bfloat16, jnp.int32
    c0 = (((0,), (0,)), ((), ()))
    c1 = (((1,), (1,)), ((), ()))
    right = [(i, (i + 2) % ntp) for i in range(ntp)]
    left = [(i, (i - 2) % ntp) for i in range(ntp)]
    twin = [(i, i ^ 1) for i in range(ntp)]

    def dot(a, b, dims=(((1,), (0,)), ((), ()))):
        return lax.dot_general(a, b, dims, preferred_element_type=f32)

    def send(a, ring, axis="tp"):
        return lax.ppermute(a, axis, ring)

    def mm(*a):
        return dot(*a).astype(bf16)

    def tie(a, b):
        return lax.optimization_barrier((a, b))[0]

    def work(ids, E, g, W, du, dres):
        vs, d = E.shape
        nk, t = ids.shape
        ts = t // ntp
        fs = W.shape[1]
        nt = nk * t
        nl = nk * ts
        me = lax.axis_index("tp")
        ch, co = me // 2, me % 2
        lo = me * vs
        gf = g.astype(f32)

        sizes = (nk // 4, nk // 2, nk // 4)
        starts = (0, nk // 4, 3 * nk // 4)
        nc = len(sizes)

        def pick(a, chip, core, k0, k1):
            return lax.dynamic_slice(a, (k0, chip % nch, core, 0, 0), (k1 - k0, 1, 1, ts, d)).reshape(k1 - k0, ts, d).astype(f32)

        def pick1(a, chip, k0, k1):
            return lax.dynamic_slice(a, (k0, chip % nch, 0, 0), (k1 - k0, 1, ts, d)).reshape(k1 - k0, ts, d).astype(f32)

        ps, gots, near = [], [], []

        def term(c, chip, k0, k1):
            return pick(ps[c], chip, co, k0, k1) + pick1(gots[c], chip, k0, k1)

        def after(c, x):
            ps[c], gots[c], _ = lax.optimization_barrier((ps[c], gots[c], x))

        def spread(c):
            kc, ka = sizes[c], sizes[c] // 2
            to_r = jnp.concatenate([term(c, ch + 2, 0, ka), term(c, ch + 1, ka, kc)], axis=0)
            to_l = jnp.concatenate([term(c, ch + nch - 1, 0, ka), term(c, ch + 2, ka, kc)], axis=0)
            to_r, to_l = lax.optimization_barrier((to_r, to_l))
            near.append((send(to_r, right), send(to_l, left)))
            return to_l

        for c in range(nc):
            kc = sizes[c]
            a = du[starts[c]:starts[c] + kc].reshape(kc * t, fs)
            p = mm(a, W, c1).reshape(kc, nch, 2, ts, d)
            other = lax.dynamic_slice(p, (0, 0, 1 - co, 0, 0), (kc, nch, 1, ts, d)).reshape(kc, nch, ts, d)
            ps.append(p)
            gots.append(send(other, twin))
        for c in range(nc):
            last = spread(c)

        relay = []

        def pass_on(c, chip):
            kc, ka = sizes[c], sizes[c] // 2
            qa = term(c, chip + 1, 0, ka) + near[c][0][:ka]
            qb = term(c, chip + nch - 1, ka, kc) + near[c][1][ka:]
            relay.append((send(qa, right), send(qb, left)))

        after(0, last)
        pass_on(0, ch)

        idf = ids.reshape(-1)
        nhi = ntp * vs // LANES
        per = vs // LANES
        ohi = (idf[:, None] // LANES == lax.broadcasted_iota(i32, (nt, nhi), 1)).astype(bf16)
        olo = (idf[:, None] % LANES == lax.broadcasted_iota(i32, (nt, LANES), 1)).astype(bf16)
        pres = (dot(ohi, olo, c0) > 0).astype(bf16)
        r0 = lax.broadcasted_iota(i32, (LANES, LANES), 0)
        r1 = lax.broadcasted_iota(i32, (LANES, LANES), 1)
        within = dot(pres, (r0 < r1).astype(bf16))
        h0 = lax.broadcasted_iota(i32, (nhi, nhi), 0)
        h1 = lax.broadcasted_iota(i32, (nhi, nhi), 1)
        above = dot(((h1 < h0) & (h0 // per == h1 // per)).astype(bf16), jnp.sum(pres.astype(f32), axis=1, keepdims=True).astype(bf16))
        smap = (within + above).astype(i32)
        s_hi, s_lo = (smap // LANES).astype(bf16), (smap % LANES).astype(bf16)
        slot = jnp.sum((dot(ohi, s_hi) * LANES + dot(ohi, s_lo)) * olo.astype(f32), axis=1).astype(i32)
        own = idf // vs
        away = (own // 2 + nch - ch) % nch
        place = jnp.where(own % 2 == co, 0, nch) + jnp.where(away == 0, 0, jnp.where(away == nch - 1, 1, away + 1))
        idh = ids.reshape(nk, ntp, ts).transpose(1, 0, 2).reshape(ntp, nl)
        ownh = idh // vs
        oc = (ownh[:, None, :] == lax.broadcasted_iota(i32, (ntp, ntp, nl), 1)).astype(bf16).reshape(ntp * ntp, nl)
        j0 = lax.broadcasted_iota(i32, (nl, nl), 0)
        j1 = lax.broadcasted_iota(i32, (nl, nl), 1)
        before = dot(oc, (j0 < j1).astype(bf16))
        rank = jnp.sum((before * oc.astype(f32)).reshape(ntp, ntp, nl), axis=1).astype(i32)

        rmax = jnp.stack([jnp.max(slot) // ROWS, jnp.max(rank) // CAP]) + 1
        step = 1
        while step < mesh.shape["dp"]:
            ring = [(i, (i + step) % mesh.shape["dp"]) for i in range(mesh.shape["dp"])]
            rmax = jnp.maximum(rmax, send(rmax, ring, "dp"))
            step *= 2
        rounds, xrounds = rmax[0], rmax[1]

        sm_me = lax.dynamic_slice_in_dim(jnp.where(pres > 0, smap, -1), me * per, per, 0).reshape(vs)

        def gather_round(r, wait_for=None):
            hit = lax.broadcasted_iota(i32, (ROWS, vs), 0) == (sm_me - r * ROWS)[None, :]
            rows = jnp.sum(jnp.where(hit, lax.broadcasted_iota(i32, (ROWS, vs), 1), 0), axis=1)
            x0 = jnp.take(E, rows, axis=0, mode="clip")
            x1, x2 = send(x0, right), send(x0, left)
            x3 = [send(x1[:ROWS // 2], right), send(x2[ROWS // 2:], left)]
            lane = jnp.concatenate([x0, x1, x2] + x3, axis=0)
            xt = jnp.concatenate([lane, send(lane, twin)], axis=0)
            if wait_for is not None:
                xt = tie(xt, wait_for)
            xf = xt.astype(f32)
            rs = lax.rsqrt(jnp.mean(xf * xf, axis=-1, keepdims=True) + EPS)
            ntab = ((xf * rs) * gf).astype(bf16)
            key = slot - r * ROWS
            tix = jnp.where((key >= 0) & (key < ROWS), place * ROWS + key, -1)
            oht = (tix[:, None] == lax.broadcasted_iota(i32, (nt, ntp * ROWS), 1)).astype(bf16)
            n = mm(oht, ntab)
            tih = lax.dynamic_slice_in_dim(tix.reshape(nk, t), me * ts, ts, 1).reshape(-1)
            ohh = (tih[:, None] == lax.broadcasted_iota(i32, (nl, ntp * ROWS), 1)).astype(bf16)
            return n, dot(ohh, xt).astype(bf16)

        def more(c):
            r, n, xl = c
            n2, xl2 = gather_round(r)
            return r + 1, n + n2, xl + xl2

        n, xl = gather_round(0, last)
        _, n, xl = lax.while_loop(lambda c: c[0] < rounds, more, (i32(1), n, xl))

        for c in range(1, nc):
            after(c, n)
            pass_on(c, ch)
        u = mm(n, W)
        for c in range(nc):
            after(c, (relay[c], u))
        dns = []
        for c in range(nc):
            kc, ka = sizes[c], sizes[c] // 2
            dns.append(term(c, ch, 0, ka) + relay[c][0] + near[c][1][:ka])
            dns.append(term(c, ch, ka, kc) + near[c][0][ka:] + relay[c][1])
        dn = jnp.concatenate(dns, axis=0).reshape(nl, d)

        xf = xl.astype(f32)
        rs = lax.rsqrt(jnp.mean(xf * xf, axis=-1, keepdims=True) + EPS)
        nh = xf * rs
        gdn = gf * dn
        dx = dres.reshape(nl, d).astype(f32) + rs * (gdn - nh * jnp.mean(nh * gdn, axis=-1, keepdims=True))
        dxb = dx.astype(bf16)
        dgp = jnp.sum(dn * nh, axis=0)

        ownm = lax.dynamic_index_in_dim(ownh, me, 0, keepdims=False)
        rankm = lax.dynamic_index_in_dim(rank, me, 0, keepdims=False)

        def send_round(r):
            key = rankm - r * CAP
            q = jnp.where((key >= 0) & (key < CAP), ownm * CAP + key, -1)
            oh = (lax.broadcasted_iota(i32, (ntp * CAP, nl), 0) == q[None, :]).astype(bf16)
            b = dot(oh, dxb).astype(bf16)
            got = lax.all_to_all(b.reshape(ntp, CAP, d), "tp", 0, 0, tiled=True).reshape(ntp * CAP, d)
            sends.append((b, got))
            hit = (ownh == me)[:, None, :] & ((rank - r * CAP)[:, None, :] == lax.broadcasted_iota(i32, (ntp, CAP, nl), 1))
            rows = (jnp.sum(jnp.where(hit, (idh - lo + 1)[:, None, :], 0), axis=2) - 1).reshape(-1)
            ohr = (lax.broadcasted_iota(i32, (vs, ntp * CAP), 0) == rows[None, :]).astype(bf16)
            return dot(ohr, got)

        sends = []
        dE = send_round(0)
        dW = dot(n, du.reshape(nt, fs), c0)
        dgp = tie(dgp, sends[0][1])
        dg = jnp.sum(lax.all_to_all(jnp.broadcast_to(dgp, (ntp, d)), "tp", 0, 0, tiled=True), axis=0)
        _, dE = lax.while_loop(lambda c: c[0] < xrounds, lambda c: (c[0] + 1, c[1] + send_round(c[0])), (i32(1), dE))
        return u.reshape(nk, t, fs), xl.reshape(nk, ts, d), dE, dW, dg


    return jax.shard_map(
        work,
        mesh=mesh,
        in_specs=(P("dp", None), P("tp", None), P(None), P(None, "tp"), P("dp", None, "tp"), P("dp", "tp", None)),
        out_specs=(P("dp", None, "tp"), P("dp", "tp", None), P(("dp", "tp"), None), P("dp", "tp"), P("dp")),
        check_vma=False,
    )
```

profile of v0, /device:TPU:112, one launch (start us, length us, event | category | flops | bytes accessed | tf_op | source)
XLA Modules:
  0.0 483.1 jit_solution(2098224846203986862)
XLA Ops:
  3.7 8.5 %gather_fusion.1 = bf16[176,3072]{1,0:T(8,128)(2,1)S(1)} fusion(bf16[2048,3072]{1,0:T(8,128)(2,1)} %param.11, s32[1024]{0:T(1024)S(1)} %pad_clamp_fusion.1), kind=kCustom, calls=%fused_computation.1 | custom fusion | bytes 2163392 | tf_op jit(solution)/shard_map/jit(_take)/gather | solution.py:133
  16.3 6.0 %fusion.125 = (bf16[4,256,1536]{2,1,0:T(8,128)(2,1)}, bf16[4,256,1536]{2,1,0:T(8,128)(2,1)}) fusion(bf16[16,256,1536]{2,1,0:T(8,128)(2,1)} %param.14), kind=kLoop, calls=%fused_computation.320 | loop fusion | bytes 12582912 | tf_op jit(solution)/shard_map/slice | solution.py:75
  22.3 15.7 %convolution_convert_fusion.5 = bf16[1024,3072]{1,0:T(8,128)(2,1)} fusion(bf16[1024,1536]{1,0:T(8,128)(2,1)} %bitcast.275, bf16[3072,1536]{1,0:T(8,128)(2,1)} %param.13), kind=kOutput, calls=%fused_computation.79 | convolution fusion | flops 9666822144 | bytes 18874368 | tf_op jit(solution)/shard_map/dot_general | solution.py:24
  38.0 3.9 copy_bitcast_fusion.2
  41.9 12.5 %convolution_convert_fusion.4 = bf16[1024,3072]{1,0:T(8,128)(2,1)S(1)} fusion(bf16[1024,1536]{1,0:T(8,128)(2,1)S(1)} %bitcast.274, bf16[3072,1536]{1,0:T(8,128)(2,1)} %param.13), kind=kOutput, calls=%fused_computation.78 | convolution fusion | flops 9666822144 | bytes 18874368 | tf_op jit(solution)/shard_map/dot_general | solution.py:24
  61.7 6.0 %slice.76 = bf16[8,256,1536]{2,1,0:T(8,128)(2,1)} slice(bf16[16,256,1536]{2,1,0:T(8,128)(2,1)} %param.14), slice={[4:12], [0:256], [0:1536]} | slice | bytes 12582912 | tf_op jit(solution)/shard_map/slice | solution.py:75
  69.1 26.4 %convolution_convert_fusion.3 = bf16[2048,3072]{1,0:T(8,128)(2,1)} fusion(bf16[2048,1536]{1,0:T(8,128)(2,1)} %bitcast.262, bf16[3072,1536]{1,0:T(8,128)(2,1)} %param.13), kind=kOutput, calls=%fused_computation.59 | convolution fusion | flops 19333644288 | bytes 28311552 | tf_op jit(solution)/shard_map/dot_general | solution.py:24
  104.9 8.9 %collective-permute-done.7 = bf16[88,3072]{1,0:T(8,128)(2,1)S(1)} collective-permute-done((bf16[88,3072]{1,0:T(8,128)(2,1)S(1)}, bf16[88,3072]{1,0:T(8,128)(2,1)S(1)}, u32[]{:S(2)}, u32[]{:S(2)}) %collective-permute-start.7) | collective-permute-done | bytes 540704 | tf_op jit(solution)/shard_map/ppermute | solution.py:27
  127.5 6.2 %copy_bitcast_fusion = bf16[8,4,32,3072]{3,2,0,1:T(8,128)(2,1)} fusion(bf16[8,4,2,32,3072]{4,3,2,1,0:T(8,128)(2,1)} %bitcast.257, s32[]{:T(128)S(6)} %select_n.440), kind=kLoop, calls=%fused_computation.75 | loop fusion | bytes 12582916 | tf_op jit(solution)/shard_map/reshape | solution.py:77
  142.5 3.2 collective-permute-start.24
  145.7 17.0 %collective-permute-done.15 = f32[4,32,3072]{2,1,0:T(8,128)S(1)} collective-permute-done((f32[4,32,3072]{2,1,0:T(8,128)S(1)}, f32[4,32,3072]{2,1,0:T(8,128)S(1)}, u32[]{:S(2)}, u32[]{:S(2)}) %collective-permute-start.15) | collective-permute-done | bytes 1572896 | tf_op jit(solution)/shard_map/ppermute | solution.py:27
  165.2 3.4 slice_add_fusion.10
  168.6 4.6 constant_dynamic-update-slice_fusion.16
  173.2 5.2 %fusion.15 = f32[1408]{0:T(1024)S(1)} fusion(bf16[1408,3072]{1,0:T(8,128)(2,1)} %constant_dynamic-update-slice_fusion.16), kind=kLoop, calls=%fused_computation.54 | loop fusion | flops 12974720 | bytes 8656384 | tf_op jit(solution)/shard_map/reduce_sum | solution.py:141
  178.4 10.0 %convolution_convert_fusion.7 = bf16[512,3072]{1,0:T(8,128)(2,1)} fusion(bf16[1408,3072]{1,0:T(8,128)(2,1)} %constant_dynamic-update-slice_fusion.16, s32[512]{0:T(512)S(1)} %eq.306), kind=kOutput, calls=%fused_computation.84 | convolution fusion | flops 4431478784 | bytes 11798528 | tf_op jit(solution)/shard_map/dot_general | solution.py:24
  188.3 46.4 %fusion.14 = bf16[4096,3072]{1,0:T(8,128)(2,1)} fusion(s32[4096]{0:T(1024)S(1)} %get-tuple-element.362, bf16[1408,3072]{1,0:T(8,128)(2,1)} %constant_dynamic-update-slice_fusion.16, f32[3072]{0:T(1024)S(1)} %convert_element_type.441, f32[1408]{0:T(1024)S(1)} %add_rsqrt_fusion.1), kind=kOutput, calls=%fused_computation.51 | convolution fusion | flops 35469131776 | bytes 33850880 | tf_op jit(solution)/shard_map/dot_general | solution.py:24
  234.8 10.1 %while.26 = (s32[]{:T(128)}, bf16[4096,3072]{1,0:T(8,128)(2,1)}, bf16[512,3072]{1,0:T(8,128)(2,1)}, s32[]{:T(128)}, s32[4096]{0:T(1024)S(1)}, /*index=5*/s32[409...) while((s32[]{:T(128)}, bf16[4096,3072]{1,0:T(8,128)(2,1)}, ...), condition=%wide.region_10.11_spmd, body=%wide.region_7.10_spmd.sunk | while | flops 39928856576 | bytes 164145616 | solution.py:157
  245.0 3.2 collective-permute-start.16
  248.2 4.0 convert_add_fusion.5
  252.8 12.2 %collective-permute-done.14 = f32[2,32,3072]{2,1,0:T(8,128)S(1)} collective-permute-done((f32[2,32,3072]{2,1,0:T(8,128)S(1)}, f32[2,32,3072]{2,1,0:T(8,128)S(1)}, u32[]{:S(2)}, u32[]{:S(2)}) %collective-permute-start.14) | collective-permute-done | bytes 786464 | tf_op jit(solution)/shard_map/ppermute | solution.py:27
  265.0 46.7 %convolution_convert_fusion.2 = bf16[4096,1536]{1,0:T(8,128)(2,1)} fusion(bf16[4096,3072]{1,0:T(8,128)(2,1)} %get-tuple-element.290, bf16[3072,1536]{1,0:T(8,128)(2,1)} %param.13), kind=kOutput, calls=%fused_computation.57 | convolution fusion | flops 38660997120 | bytes 47185920 | tf_op jit(solution)/shard_map/dot_general | solution.py:24
  318.1 15.4 %collective-permute-done.20 = f32[8,32,3072]{2,1,0:T(8,128)S(1)} collective-permute-done((f32[8,32,3072]{2,1,0:T(8,128)S(1)}, f32[8,32,3072]{2,1,0:T(8,128)S(1)}, u32[]{:S(2)}, u32[]{:S(2)}) %collective-permute-start.20) | collective-permute-done | bytes 3145760 | tf_op jit(solution)/shard_map/ppermute | solution.py:27
  333.6 3.6 collective-permute-done.18
  339.8 3.2 collective-permute-start.21
  345.6 8.4 %collective-permute-done.23 = f32[2,32,3072]{2,1,0:T(8,128)S(1)} collective-permute-done((f32[2,32,3072]{2,1,0:T(8,128)S(1)}, f32[2,32,3072]{2,1,0:T(8,128)S(1)}, u32[]{:S(2)}, u32[]{:S(2)}) %collective-permute-start.23) | collective-permute-done | bytes 786464 | tf_op jit(solution)/shard_map/ppermute | solution.py:27
  354.0 31.2 %collective-permute-done.19 = f32[4,32,3072]{2,1,0:T(8,128)S(1)} collective-permute-done((f32[4,32,3072]{2,1,0:T(8,128)S(1)}, f32[4,32,3072]{2,1,0:T(8,128)S(1)}, u32[]{:S(2)}, u32[]{:S(2)}) %collective-permute-start.19) | collective-permute-done | bytes 1572896 | tf_op jit(solution)/shard_map/ppermute | solution.py:27
  397.0 4.4 convolution_convert_fusion.6
  401.4 4.8 all-to-all-start.1
  406.2 48.6 %fusion.127 = f32[3072,1536]{1,0:T(8,128)} fusion(bf16[4096,3072]{1,0:T(8,128)(2,1)} %get-tuple-element.290, bf16[4096,1536]{1,0:T(8,128)(2,1)} %bitcast.256), kind=kOutput, calls=%fused_computation.322 | convolution fusion | flops 38654705664 | bytes 56623104 | tf_op jit(solution)/shard_map/dot_general | solution.py:24
  454.8 6.5 %all-to-all-done.1 = bf16[8,96,3072]{2,1,0:T(8,128)(2,1)} async-done(((bf16[8,96,3072]{2,1,0:T(8,128)(2,1)}), bf16[8,96,3072]{2,1,0:T(8,128)(2,1)}, u32[]{:S(2)}, u32[]{:S(2)}) %all-to-all-start.1) | async-done | bytes 4718624 | tf_op jit(solution)/shard_map/all_to_all | solution.py:188
  462.1 3.8 all-to-all-start.2
  465.9 15.6 %fusion.32 = f32[2048,3072]{1,0:T(8,128)} fusion(bf16[768,3072]{1,0:T(8,128)(2,1)} %bitcast.74, s32[768]{0:T(1024)S(1)} %copy-done.25), kind=kOutput, calls=%fused_computation.77 | convolution fusion | flops 9665249280 | bytes 29887488 | tf_op jit(solution)/shard_map/dot_general | solution.py:24
  (151 shorter events, 72.0 us)
Async XLA Ops:
  12.2 86.0 %collective-permute-start.5 = (bf16[176,3072]{1,0:T(8,128)(2,1)S(1)}, bf16[176,3072]{1,0:T(8,128)(2,1)S(1)}, u32[]{:S(2)}, u32[]{:S(2)}) collective-permute-start(bf16[176,3072]{1,0:T(8,128)(2,1)S(1)} %gather_fusion.1), channel_id=1, source_target_pairs={{0,2},{1,3},{2,4},{3,5},{4,6},{5,7},{6,0},{7,1},{8,10},{9,11},{10,... | collective-permute-start | bytes 3244040 | tf_op jit(solution)/shard_map/ppermute | solution.py:27
  14.7 84.1 %collective-permute-start.6 = (bf16[176,3072]{1,0:T(8,128)(2,1)S(1)}, bf16[176,3072]{1,0:T(8,128)(2,1)S(1)}, u32[]{:S(2)}, u32[]{:S(2)}) collective-permute-start(bf16[176,3072]{1,0:T(8,128)(2,1)S(1)} %gather_fusion.1), channel_id=1, source_target_pairs={{0,6},{1,7},{2,0},{3,1},{4,2},{5,3},{6,4},{7,5},{8,14},{9,15},{10,... | collective-permute-start | bytes 3244040 | tf_op jit(solution)/shard_map/ppermute | solution.py:27
  41.9 96.2 %collective-permute-start.10 = (bf16[4,4,32,3072]{3,2,0,1:T(8,128)(2,1)}, bf16[4,4,32,3072]{3,2,0,1:T(8,128)(2,1)}, u32[]{:S(2)}, u32[]{:S(2)}) collective-permute-start(bf16[4,4,32,3072]{3,2,0,1:T(8,128)(2,1)} %copy_bitcast_fusion.2), channel_id=1, source_target_pairs={{0,1},{1,0},{2,3},{3,2},{4,5},{5,4},{6,7},{7,6},{8,9},{9,8},{10,11... | collective-permute-start | bytes 9437192 | tf_op jit(solution)/shard_map/ppermute | solution.py:27
  59.0 63.7 %collective-permute-start.12 = (bf16[4,4,32,3072]{3,2,0,1:T(8,128)(2,1)}, bf16[4,4,32,3072]{3,2,0,1:T(8,128)(2,1)}, u32[]{:S(2)}, u32[]{:S(2)}) collective-permute-start(bf16[4,4,32,3072]{3,2,0,1:T(8,128)(2,1)} %copy_bitcast_fusion.1), channel_id=1, source_target_pairs={{0,1},{1,0},{2,3},{3,2},{4,5},{5,4},{6,7},{7,6},{8,9},{9,8},{10,11... | collective-permute-start | bytes 9437192 | tf_op jit(solution)/shard_map/ppermute | solution.py:27
  69.1 51.8 %copy-start.11 = (s32[8,512]{1,0:T(8,128)}, s32[8,512]{1,0:T(8,128)S(1)}, u32[]{:S(2)}) copy-start(s32[8,512]{1,0:T(8,128)S(1)} %reshape.570) | copy-start | bytes 49156
  69.1 53.0 %copy-start.17 = (s32[8,512]{1,0:T(8,128)}, s32[8,512]{1,0:T(8,128)S(1)}, u32[]{:S(2)}) copy-start(s32[8,512]{1,0:T(8,128)S(1)} %get-tuple-element.617) | copy-start | bytes 49156
  98.3 15.5 %collective-permute-start.7 = (bf16[88,3072]{1,0:T(8,128)(2,1)S(1)}, bf16[88,3072]{1,0:T(8,128)(2,1)S(1)}, u32[]{:S(2)}, u32[]{:S(2)}) collective-permute-start(bf16[88,3072]{1,0:T(8,128)(2,1)S(1)} %slice.92), channel_id=1, source_target_pairs={{0,2},{1,3},{2,4},{3,5},{4,6},{5,7},{6,0},{7,1},{8,10},{9,11},{10,... | collective-permute-start | bytes 1622024 | tf_op jit(solution)/shard_map/ppermute | solution.py:27
  98.8 16.1 %collective-permute-start.8 = (bf16[88,3072]{1,0:T(8,128)(2,1)S(1)}, bf16[88,3072]{1,0:T(8,128)(2,1)S(1)}, u32[]{:S(2)}, u32[]{:S(2)}) collective-permute-start(bf16[88,3072]{1,0:T(8,128)(2,1)S(1)} %slice.93), channel_id=1, source_target_pairs={{0,6},{1,7},{2,0},{3,1},{4,2},{5,3},{6,4},{7,5},{8,14},{9,15},{10,... | collective-permute-start | bytes 1622024 | tf_op jit(solution)/shard_map/ppermute | solution.py:27
  101.7 19.0 %copy-start.24 = (bf16[3072]{0:T(1024)(128)(2,1)S(1)}, bf16[3072]{0:T(1024)(128)(2,1)}, u32[]{:S(2)}) copy-start(bf16[3072]{0:T(1024)(128)(2,1)} %param.12) | copy-start | bytes 18436
  115.9 52.6 %collective-permute-start.9 = (bf16[704,3072]{1,0:T(8,128)(2,1)}, bf16[704,3072]{1,0:T(8,128)(2,1)}, u32[]{:S(2)}, u32[]{:S(2)}) collective-permute-start(bf16[704,3072]{1,0:T(8,128)(2,1)} %get-tuple-element.402), channel_id=1, source_target_pairs={{0,1},{1,0},{2,3},{3,2},{4,5},{5,4},{6,7},{7,6},{8,9},{9,8},{10,11... | collective-permute-start | bytes 12976136 | tf_op jit(solution)/shard_map/ppermute | solution.py:27
  125.4 37.3 %collective-permute-start.15 = (f32[4,32,3072]{2,1,0:T(8,128)S(1)}, f32[4,32,3072]{2,1,0:T(8,128)S(1)}, u32[]{:S(2)}, u32[]{:S(2)}) collective-permute-start(f32[4,32,3072]{2,1,0:T(8,128)S(1)} %get-tuple-element.295), channel_id=1, source_target_pairs={{0,6},{1,7},{2,0},{3,1},{4,2},{5,3},{6,4},{7,5},{8,14},{9,15},{10,... | collective-permute-start | bytes 4718600 | tf_op jit(solution)/shard_map/ppermute | solution.py:27
  127.5 37.7 %collective-permute-start.13 = (f32[4,32,3072]{2,1,0:T(8,128)S(1)}, f32[4,32,3072]{2,1,0:T(8,128)S(1)}, u32[]{:S(2)}, u32[]{:S(2)}) collective-permute-start(f32[4,32,3072]{2,1,0:T(8,128)S(1)} %get-tuple-element.294), channel_id=1, source_target_pairs={{0,2},{1,3},{2,4},{3,5},{4,6},{5,7},{6,0},{7,1},{8,10},{9,11},{10,... | collective-permute-start | bytes 4718600 | tf_op jit(solution)/shard_map/ppermute | solution.py:27
  133.7 3.7 collective-permute-start.11
  138.1 110.1 %collective-permute-start.17 = (bf16[8,4,32,3072]{3,2,0,1:T(8,128)(2,1)}, bf16[8,4,32,3072]{3,2,0,1:T(8,128)(2,1)}, u32[]{:S(2)}, u32[]{:S(2)}) collective-permute-start(bf16[8,4,32,3072]{3,2,0,1:T(8,128)(2,1)} %copy_bitcast_fusion), channel_id=1, source_target_pairs={{0,1},{1,0},{2,3},{3,2},{4,5},{5,4},{6,7},{7,6},{8,9},{9,8},{10,11... | collective-permute-start | bytes 18874376 | tf_op jit(solution)/shard_map/ppermute | solution.py:27
  142.5 169.2 %collective-permute-start.24 = (f32[4,32,3072]{2,1,0:T(8,128)}, f32[4,32,3072]{2,1,0:T(8,128)}, u32[]{:S(2)}, u32[]{:S(2)}) collective-permute-start(f32[4,32,3072]{2,1,0:T(8,128)} %get-tuple-element.288), channel_id=1, source_target_pairs={{0,6},{1,7},{2,0},{3,1},{4,2},{5,3},{6,4},{7,5},{8,14},{9,15},{10,... | collective-permute-start | bytes 4718600 | tf_op jit(solution)/shard_map/ppermute | solution.py:27
  162.8 149.0 %collective-permute-start.22 = (f32[4,32,3072]{2,1,0:T(8,128)}, f32[4,32,3072]{2,1,0:T(8,128)}, u32[]{:S(2)}, u32[]{:S(2)}) collective-permute-start(f32[4,32,3072]{2,1,0:T(8,128)} %get-tuple-element.306), channel_id=1, source_target_pairs={{0,2},{1,3},{2,4},{3,5},{4,6},{5,7},{6,0},{7,1},{8,10},{9,11},{10,... | collective-permute-start | bytes 4718600 | tf_op jit(solution)/shard_map/ppermute | solution.py:27
  188.3 46.4 %copy-start.20 = (s32[2048]{0:T(1024)S(1)}, s32[2048]{0:T(1024)}, u32[]{:S(2)}) copy-start(s32[2048]{0:T(1024)} %copy-done.19) | copy-start | bytes 24580
  244.9 20.1 %collective-permute-start.14 = (f32[2,32,3072]{2,1,0:T(8,128)S(1)}, f32[2,32,3072]{2,1,0:T(8,128)S(1)}, u32[]{:S(2)}, u32[]{:S(2)}) collective-permute-start(f32[2,32,3072]{2,1,0:T(8,128)S(1)} %copy-done.16), channel_id=1, source_target_pairs={{0,2},{1,3},{2,4},{3,5},{4,6},{5,7},{6,0},{7,1},{8,10},{9,11},{10,... | collective-permute-start | bytes 2359304 | tf_op jit(solution)/shard_map/ppermute | solution.py:27
  245.0 66.7 %collective-permute-start.16 = (f32[2,32,3072]{2,1,0:T(8,128)S(1)}, f32[2,32,3072]{2,1,0:T(8,128)S(1)}, u32[]{:S(2)}, u32[]{:S(2)}) collective-permute-start(f32[2,32,3072]{2,1,0:T(8,128)S(1)} %copy-done.15), channel_id=1, source_target_pairs={{0,6},{1,7},{2,0},{3,1},{4,2},{5,3},{6,4},{7,5},{8,14},{9,15},{10,... | collective-permute-start | bytes 2359304 | tf_op jit(solution)/shard_map/ppermute | solution.py:27
  252.6 80.9 %collective-permute-start.20 = (f32[8,32,3072]{2,1,0:T(8,128)S(1)}, f32[8,32,3072]{2,1,0:T(8,128)S(1)}, u32[]{:S(2)}, u32[]{:S(2)}) collective-permute-start(f32[8,32,3072]{2,1,0:T(8,128)S(1)} %get-tuple-element.301), channel_id=1, source_target_pairs={{0,6},{1,7},{2,0},{3,1},{4,2},{5,3},{6,4},{7,5},{8,14},{9,15},{10,... | collective-permute-start | bytes 9437192 | tf_op jit(solution)/shard_map/ppermute | solution.py:27
  265.0 72.2 %collective-permute-start.18 = (f32[8,32,3072]{2,1,0:T(8,128)S(1)}, f32[8,32,3072]{2,1,0:T(8,128)S(1)}, u32[]{:S(2)}, u32[]{:S(2)}) collective-permute-start(f32[8,32,3072]{2,1,0:T(8,128)S(1)} %get-tuple-element.300), channel_id=1, source_target_pairs={{0,2},{1,3},{2,4},{3,5},{4,6},{5,7},{6,0},{7,1},{8,10},{9,11},{10,... | collective-permute-start | bytes 9437192 | tf_op jit(solution)/shard_map/ppermute | solution.py:27
  314.0 40.0 %collective-permute-start.23 = (f32[2,32,3072]{2,1,0:T(8,128)S(1)}, f32[2,32,3072]{2,1,0:T(8,128)S(1)}, u32[]{:S(2)}, u32[]{:S(2)}) collective-permute-start(f32[2,32,3072]{2,1,0:T(8,128)S(1)} %get-tuple-element.385), channel_id=1, source_target_pairs={{0,2},{1,3},{2,4},{3,5},{4,6},{5,7},{6,0},{7,1},{8,10},{9,11},{10,... | collective-permute-start | bytes 2359304 | tf_op jit(solution)/shard_map/ppermute | solution.py:27
  314.6 39.5 %collective-permute-start.25 = (f32[2,32,3072]{2,1,0:T(8,128)S(1)}, f32[2,32,3072]{2,1,0:T(8,128)S(1)}, u32[]{:S(2)}, u32[]{:S(2)}) collective-permute-start(f32[2,32,3072]{2,1,0:T(8,128)S(1)} %get-tuple-element.384), channel_id=1, source_target_pairs={{0,6},{1,7},{2,0},{3,1},{4,2},{5,3},{6,4},{7,5},{8,14},{9,15},{10,... | collective-permute-start | bytes 2359304 | tf_op jit(solution)/shard_map/ppermute | solution.py:27
  318.1 24.9 %copy-start.10 = (f32[4,32,3072]{2,1,0:T(8,128)S(1)}, f32[4,32,3072]{2,1,0:T(8,128)}, u32[]{:S(2)}) copy-start(f32[4,32,3072]{2,1,0:T(8,128)} %copy-done.9) | copy-start | bytes 4718596
  318.1 26.2 %copy-start.8 = (f32[4,32,3072]{2,1,0:T(8,128)S(1)}, f32[4,32,3072]{2,1,0:T(8,128)}, u32[]{:S(2)}) copy-start(f32[4,32,3072]{2,1,0:T(8,128)} %copy-done.7) | copy-start | bytes 4718596
  339.7 45.6 %collective-permute-start.19 = (f32[4,32,3072]{2,1,0:T(8,128)S(1)}, f32[4,32,3072]{2,1,0:T(8,128)S(1)}, u32[]{:S(2)}, u32[]{:S(2)}) collective-permute-start(f32[4,32,3072]{2,1,0:T(8,128)S(1)} %get-tuple-element.377), channel_id=1, source_target_pairs={{0,2},{1,3},{2,4},{3,5},{4,6},{5,7},{6,0},{7,1},{8,10},{9,11},{10,... | collective-permute-start | bytes 4718600 | tf_op jit(solution)/shard_map/ppermute | solution.py:27
  339.8 45.5 %collective-permute-start.21 = (f32[4,32,3072]{2,1,0:T(8,128)S(1)}, f32[4,32,3072]{2,1,0:T(8,128)S(1)}, u32[]{:S(2)}, u32[]{:S(2)}) collective-permute-start(f32[4,32,3072]{2,1,0:T(8,128)S(1)} %get-tuple-element.376), channel_id=1, source_target_pairs={{0,6},{1,7},{2,0},{3,1},{4,2},{5,3},{6,4},{7,5},{8,14},{9,15},{10,... | collective-permute-start | bytes 4718600 | tf_op jit(solution)/shard_map/ppermute | solution.py:27
  401.4 59.9 %all-to-all-start.1 = ((bf16[8,96,3072]{2,1,0:T(8,128)(2,1)}), bf16[8,96,3072]{2,1,0:T(8,128)(2,1)}, u32[]{:S(2)}, u32[]{:S(2)}) async-start(bf16[8,96,3072]{2,1,0:T(8,128)(2,1)} %bitcast.273), calls=%async_computation.1 | async-start | bytes 9437184 | tf_op jit(solution)/shard_map/all_to_all | solution.py:188
  406.2 59.6 %copy-start.25 = (s32[768]{0:T(1024)S(1)}, s32[768]{0:T(1024)}, u32[]{:S(2)}) copy-start(s32[768]{0:T(1024)} %sub.188) | copy-start | bytes 9220
  462.1 19.4 %all-to-all-start.2 = ((f32[8,1,3072]{2,1,0:T(1,128)}), f32[8,1,3072]{2,1,0:T(1,128)S(1)}, u32[]{:S(2)}, u32[]{:S(2)}) async-start(f32[8,1,3072]{2,1,0:T(1,128)} %broadcast_in_dim.108), calls=%async_computation.2 | async-start | bytes 196608 | tf_op jit(solution)/shard_map/all_to_all | solution.py:199
  465.9 16.3 %copy-start.12 = (s32[8,512]{1,0:T(8,128)S(1)}, s32[8,512]{1,0:T(8,128)}, u32[]{:S(2)}) copy-start(s32[8,512]{1,0:T(8,128)} %copy-done.11) | copy-start | bytes 49156
  465.9 16.3 %copy-start.14 = (s32[8,512]{1,0:T(8,128)S(1)}, s32[8,512]{1,0:T(8,128)}, u32[]{:S(2)}) copy-start(s32[8,512]{1,0:T(8,128)} %copy-done.13) | copy-start | bytes 49156
  (16 other events, 123.5 us)
where the time goes:
time: 489 us; the launch traced here: 483 us
  matrix products  231 us (47%)
  waiting for transfers between devices  107 us (22%)
  local copies, waits for them, and re-layouts  50.3 us (10%)
  other arithmetic  43.5 us (9%)
  starting transfers between devices  34.2 us (7%)
  loops' own time  10.8 us (2%)
  between operations  5.53 us (1%)
    dot_general x15, matrix products, dot(): return lax.dot_general(a, b, dims, preferred_element_type=f32)  231 us
    ppermute x21, waiting for transfers between devices, send(): return lax.ppermute(a, axis, ring)  101 us
    ppermute x21, starting transfers between devices, send(): return lax.ppermute(a, axis, ring)  25.6 us
    slice x2, local copies, waits for them, and re-layouts, work(): a = du[starts[c]:starts[c] + kc].reshape(kc * t, fs)  12 us
    reshape x3, local copies, waits for them, and re-layouts, work(): lax.dynamic_slice(p, (0, 0, 1 - co, 0, 0), (kc, nch, 1, ts, d))  12 us
    another operation x1, loops' own time, work(): _, n, xl = lax.while_loop(lambda c: c[0] < rounds, more, (i32(1), n, xl))  10.1 us
  transfers between devices with their start and end apart: 23, of which 10 were waited for; matrix products, arithmetic and copies ran while one was open for 61% of the time, Pallas kernels for 0%

commit v1 on v0

--- a/solution.py
+++ b/solution.py
@@ -1,6 +1,8 @@
 import jax
 import jax.numpy as jnp
 from jax import lax
+from jax.experimental import pallas as pl
+from jax.experimental.pallas import tpu as pltpu
 from jax.sharding import PartitionSpec as P
 
 
@@ -8,6 +10,30 @@
 ROWS = 176
 CAP = 96
 LANES = 128
+
+
+def terms_kernel(co, a_ref, w_ref, keep_ref, give_ref):
+    m, t, fs = a_ref.shape
+    nch, _, ts, tn = keep_ref.shape
+    r = lax.dot_general(a_ref[...].reshape(m * t, fs), w_ref[...], (((1,), (1,)), ((), ())), preferred_element_type=jnp.float32)
+    r = r.astype(jnp.bfloat16).reshape(m, nch, 2, ts, tn)
+    north = co[0] == 1
+    for chip in range(nch):
+        keep_ref[chip] = jnp.where(north, r[:, chip, 1], r[:, chip, 0])
+        give_ref[chip] = jnp.where(north, r[:, chip, 0], r[:, chip, 1])
+
+
+def spread_kernel(ch, ar, br, al, bl, r_ref, l_ref):
+    f32 = jnp.float32
+    r_ref[...] = ar[0].astype(f32) + br[0].astype(f32)
+    l_ref[...] = al[0].astype(f32) + bl[0].astype(f32)
+
+
+def lane_kernel(x0, x1, x2, x3, x4, o_ref):
+    at = 0
+    for x in (x0, x1, x2, x3, x4):
+        o_ref[at:at + x.shape[0], :] = x[...]
+        at += x.shape[0]
 
 
 def solution(mesh):
@@ -15,7 +41,6 @@
     nch = ntp // 2
     f32, bf16, i32 = jnp.float32, jnp.bfloat16, jnp.int32
     c0 = (((0,), (0,)), ((), ()))
-    c1 = (((1,), (1,)), ((), ()))
     right = [(i, (i + 2) % ntp) for i in range(ntp)]
     left = [(i, (i - 2) % ntp) for i in range(ntp)]
     twin = [(i, i ^ 1) for i in range(ntp)]
@@ -44,39 +69,64 @@
         lo = me * vs
         gf = g.astype(f32)
 
-        sizes = (nk // 4, nk // 2, nk // 4)
-        starts = (0, nk // 4, 3 * nk // 4)
+        sizes = (nk // 2, nk // 2)
+        starts = (0, nk // 2)
         nc = len(sizes)
 
-        def pick(a, chip, core, k0, k1):
-            return lax.dynamic_slice(a, (k0, chip % nch, core, 0, 0), (k1 - k0, 1, 1, ts, d)).reshape(k1 - k0, ts, d).astype(f32)
-
         def pick1(a, chip, k0, k1):
-            return lax.dynamic_slice(a, (k0, chip % nch, 0, 0), (k1 - k0, 1, ts, d)).reshape(k1 - k0, ts, d).astype(f32)
+            return lax.dynamic_slice(a, (chip % nch, k0, 0, 0), (1, k1 - k0, ts, d)).reshape(k1 - k0, ts, d).astype(f32)
 
         ps, gots, near = [], [], []
 
         def term(c, chip, k0, k1):
-            return pick(ps[c], chip, co, k0, k1) + pick1(gots[c], chip, k0, k1)
+            return pick1(ps[c], chip, k0, k1) + pick1(gots[c], chip, k0, k1)
 
         def after(c, x):
             ps[c], gots[c], _ = lax.optimization_barrier((ps[c], gots[c], x))
 
         def spread(c):
-            kc, ka = sizes[c], sizes[c] // 2
-            to_r = jnp.concatenate([term(c, ch + 2, 0, ka), term(c, ch + 1, ka, kc)], axis=0)
-            to_l = jnp.concatenate([term(c, ch + nch - 1, 0, ka), term(c, ch + 2, ka, kc)], axis=0)
-            to_r, to_l = lax.optimization_barrier((to_r, to_l))
+            kc = sizes[c]
+            kb = 2
+            na = kc // 2 // kb
+            part = (1, kb, ts, d)
+
+            def at(a, b):
+                return pl.BlockSpec(part, lambda k, s: (lax.rem(s[0] + jnp.where(k < na, a, b), nch), k, 0, 0))
+
+            rs, ls = at(2, 1), at(nch - 1, 2)
+            out = pl.BlockSpec((kb, ts, d), lambda k, s: (k, 0, 0))
+            to_r, to_l = pl.pallas_call(
+                spread_kernel,
+                grid_spec=pltpu.PrefetchScalarGridSpec(num_scalar_prefetch=1, grid=(kc // kb,), in_specs=[rs, rs, ls, ls], out_specs=[out, out]),
+                out_shape=[jax.ShapeDtypeStruct((kc, ts, d), f32)] * 2,
+                cost_estimate=pl.CostEstimate(flops=20 * kc * ts * d, bytes_accessed=16 * kc * ts * d, transcendentals=0),
+            )(ch.reshape(1), ps[c], gots[c], ps[c], gots[c])
             near.append((send(to_r, right), send(to_l, left)))
             return to_l
 
         for c in range(nc):
             kc = sizes[c]
-            a = du[starts[c]:starts[c] + kc].reshape(kc * t, fs)
-            p = mm(a, W, c1).reshape(kc, nch, 2, ts, d)
-            other = lax.dynamic_slice(p, (0, 0, 1 - co, 0, 0), (kc, nch, 1, ts, d)).reshape(kc, nch, ts, d)
-            ps.append(p)
-            gots.append(send(other, twin))
+            half = jax.ShapeDtypeStruct((nch, kc, ts, d), bf16)
+            kb, tn = kc, d // 6
+            k0 = starts[c]
+            out = pl.BlockSpec((nch, kb, ts, tn), lambda i, j, s: (0, i, 0, j))
+            keep, give = pl.pallas_call(
+                terms_kernel,
+                grid_spec=pltpu.PrefetchScalarGridSpec(
+                    num_scalar_prefetch=1,
+                    grid=(kc // kb, d // tn),
+                    in_specs=[
+                        pl.BlockSpec((pl.Element(kb), pl.Element(t), pl.Element(fs)), lambda i, j, s, k0=k0: (k0, 0, 0)),
+                        pl.BlockSpec((tn, fs), lambda i, j, s: (j, 0)),
+                    ],
+                    out_specs=[out, out],
+                ),
+                out_shape=[half, half],
+                compiler_params=pltpu.CompilerParams(vmem_limit_bytes=48 * 1024 * 1024),
+                cost_estimate=pl.CostEstimate(flops=2 * kc * t * d * fs, bytes_accessed=4 * kc * t * d, transcendentals=0),
+            )(co.reshape(1), du, W)
+            ps.append(keep)
+            gots.append(send(give, twin))
         for c in range(nc):
             last = spread(c)
 
@@ -133,7 +183,11 @@
             x0 = jnp.take(E, rows, axis=0, mode="clip")
             x1, x2 = send(x0, right), send(x0, left)
             x3 = [send(x1[:ROWS // 2], right), send(x2[ROWS // 2:], left)]
-            lane = jnp.concatenate([x0, x1, x2] + x3, axis=0)
+            lane = pl.pallas_call(
+                lane_kernel,
+                out_shape=jax.ShapeDtypeStruct((nch * ROWS, d), bf16),
+                cost_estimate=pl.CostEstimate(flops=20 * nch * ROWS * d, bytes_accessed=4 * nch * ROWS * d, transcendentals=0),
+            )(x0, x1, x2, *x3)
             xt = jnp.concatenate([lane, send(lane, twin)], axis=0)
             if wait_for is not None:
                 xt = tie(xt, wait_for)
@@ -146,7 +200,7 @@
             n = mm(oht, ntab)
             tih = lax.dynamic_slice_in_dim(tix.reshape(nk, t), me * ts, ts, 1).reshape(-1)
             ohh = (tih[:, None] == lax.broadcasted_iota(i32, (nl, ntp * ROWS), 1)).astype(bf16)
-            return n, dot(ohh, xt).astype(bf16)
+            return n, mm(ohh, xt)
 
         def more(c):
             r, n, xl = c

time: 489 us -> 447 us (0.914)
  Pallas kernels: 0 us -> 67.6 us
  matrix products: 231 us -> 172 us
  local copies, waits for them, and re-layouts: 50.3 us -> 12.3 us
  other arithmetic: 43.5 us -> 38.6 us
    pallas_call x0 -> x5, Pallas kernels: none -> 67.6 us  [the longest x2 51.6 us: work(): pl.pallas_call(terms_kernel, grid_spec=pltpu.PrefetchScalarGridSpec(num_s...]
    dot_general x15 -> x12, matrix products: 231 us -> 172 us  [dot(): return lax.dot_general(a, b, dims, preferred_element_type=f32)]
    slice x2 -> x0, local copies, waits for them, and re-layouts: 12 us -> none  [work(): a = du[starts[c]:starts[c] + kc].reshape(kc * t, fs)]
    reshape x3 -> x0, local copies, waits for them, and re-layouts: 12 us -> none  [work(): lax.dynamic_slice(p, (0, 0, 1 - co, 0, 0), (kc, nch, 1, ts, d))]
    unnamed x55 -> x45, local copies, waits for them, and re-layouts: 9.71 us -> 1.42 us
    unnamed x5 -> x0, other arithmetic: 7.65 us -> none
    concatenate x2 -> x0, local copies, waits for them, and re-layouts: 5.67 us -> none  [the longest x1 4.57 us: gather_round(): xt = jnp.concatenate([lane, send(lane, twin)], axis=0)]
    concatenate x3 -> x1, other arithmetic: 2.81 us -> 7.77 us  [gather_round(): xt = jnp.concatenate([lane, send(lane, twin)], axis=0)]
  transfers between devices with their start and end apart: 23 -> 18, of which waited for: 10 -> 6; matrix products, arithmetic and copies ran while one was open for 61% -> 44% of each run, Pallas kernels for 0% -> 15%
where the time goes in v1:
time: 447 us; the launch traced here: 442 us
  matrix products  172 us (38%)
  waiting for transfers between devices  105 us (23%)
  Pallas kernels  67.6 us (15%)
  other arithmetic  38.6 us (9%)
  starting transfers between devices  29.4 us (7%)
  local copies, waits for them, and re-layouts  12.3 us (3%)
  loops' own time  11.2 us (3%)
  between operations  5.44 us (1%)
    dot_general x12, matrix products, dot(): return lax.dot_general(a, b, dims, preferred_element_type=f32)  172 us
    ppermute x16, waiting for transfers between devices, send(): return lax.ppermute(a, axis, ring)  98.3 us
    pallas_call x2, Pallas kernels, work(): pl.pallas_call(terms_kernel, grid_spec=pltpu.PrefetchScalarGridSpec(num_s...  51.6 us
    ppermute x16, starting transfers between devices, send(): return lax.ppermute(a, axis, ring)  20.9 us
    pallas_call x2, Pallas kernels, spread(): pl.pallas_call(spread_kernel, grid_spec=pltpu.PrefetchScalarGridSpec(num_...  11.5 us
    another operation x1, loops' own time, work(): _, n, xl = lax.while_loop(lambda c: c[0] < rounds, more, (i32(1), n, xl))  10.7 us
  transfers between devices with their start and end apart: 18, of which 6 were waited for; matrix products, arithmetic and copies ran while one was open for 44% of the time, Pallas kernels for 15%

profile of v1, /device:TPU:112, one launch (start us, length us, event | category | flops | bytes accessed | tf_op | source)
XLA Modules:
  0.0 441.5 jit_solution(13259420172519859522)
XLA Ops:
  3.3 8.5 %gather_fusion.1 = bf16[176,3072]{1,0:T(8,128)(2,1)S(1)} fusion(bf16[2048,3072]{1,0:T(8,128)(2,1)} %param.11, s32[1024]{0:T(1024)S(1)} %pad_clamp_fusion.1), kind=kCustom, calls=%fused_computation.1 | custom fusion | bytes 2163392 | tf_op jit(solution)/shard_map/jit(_take)/gather | solution.py:183
  11.9 2.4 collective-permute-start.5
  16.0 23.8 %collective-permute-done.5.x1 = bf16[176,3072]{1,0:T(8,128)(2,1)S(1)} collective-permute-done((bf16[176,3072]{1,0:T(8,128)(2,1)S(1)}, bf16[176,3072]{1,0:T(8,128)(2,1)S(1)}, u32[]{:S(2)}, u32[]{:S(2)}) %collective-permute-start.5) | collective-permute-done | bytes 1081376 | tf_op jit(solution)/shard_map/ppermute | solution.py:52
  40.2 3.1 collective-permute-start.8
  43.3 26.0 %shard_map.102 = (bf16[4,8,32,3072]{3,2,1,0:T(8,128)(2,1)}, bf16[4,8,32,3072]{3,2,1,0:T(8,128)(2,1)}) custom-call(s32[1]{0:T(128)} %bitcast.6.co, bf16[16,256,1536]{2,1,0:T(8,128)(2,1)} %a_ref.3, bf16[3072,1536]{1,0:T(8,128)(2,1)} %w_ref.3), custom_call_target="tpu_custom_call" | custom-call | flops 19327352832 | bytes 25165824 | tf_op jit(solution)/shard_map/pallas_call | solution.py:113
  69.4 4.4 %shard_map.101 = bf16[704,3072]{1,0:T(8,128)(2,1)} custom-call(bf16[176,3072]{1,0:T(8,128)(2,1)} %copy-done.8, bf16[176,3072]{1,0:T(8,128)(2,1)} %copy-done.10, bf16[176,3072]{1,0:T(8,128)(2,1)} %copy-done.11, bf16[88,3072]{1,0:T(8,128)(2,1)} %collective-permute-done.7.x3, bf16[88,3072]{1,0:T(8,128)(2,1)} %collective-permute-done.8.x4), custom_call_target="tpu_custom_call" | custom-call | flops 43253760 | bytes 8650752 | tf_op jit(solution)/shard_map/pallas_call | solution.py:186
  74.3 25.6 %shard_map.104 = (bf16[4,8,32,3072]{3,2,1,0:T(8,128)(2,1)}, bf16[4,8,32,3072]{3,2,1,0:T(8,128)(2,1)}) custom-call(s32[1]{0:T(128)} %bitcast.6.co, bf16[16,256,1536]{2,1,0:T(8,128)(2,1)} %a_ref.3, bf16[3072,1536]{1,0:T(8,128)(2,1)} %w_ref.3), custom_call_target="tpu_custom_call" | custom-call | flops 19327352832 | bytes 25165824 | tf_op jit(solution)/shard_map/pallas_call | solution.py:113
  109.1 2.1 collective-permute-start.11
  113.4 7.8 %pad_maximum_fusion.3 = bf16[1408,3072]{1,0:T(8,128)(2,1)} fusion(bf16[704,3072]{1,0:T(8,128)(2,1)} %collective-permute-done.9, bf16[704,3072]{1,0:T(8,128)(2,1)} %shard_map.101), kind=kLoop, calls=%fused_computation.51 | loop fusion | flops 17301504 | bytes 17301504 | tf_op jit(solution)/shard_map/concatenate | solution.py:191
  121.2 5.7 %shard_map.103 = (f32[8,32,3072]{2,1,0:T(8,128)}, f32[8,32,3072]{2,1,0:T(8,128)}) custom-call(s32[1]{0:T(128)} %bitcast.5.ch, bf16[4,8,32,3072]{3,2,1,0:T(8,128)(2,1)} %get-tuple-element.303.ar.al, bf16[4,8,32,3072]{3,2,1,0:T(8,128)(2,1)} %collective-permute-done.10.br.bl, bf16[4,8,32,3072]{3,2,1,0:T(8,128)(2,1)} %get-tuple-element.303.ar.al, ...), custom_call_target="tpu_custom_call" | custom-call | flops 15728640 | bytes 12582912 | tf_op jit(solution)/shard_map/pallas_call | solution.py:98
  129.0 5.8 %fusion.17 = f32[1408]{0:T(1024)S(1)} fusion(bf16[1408,3072]{1,0:T(8,128)(2,1)} %pad_maximum_fusion.3), kind=kLoop, calls=%fused_computation.46 | loop fusion | flops 12974720 | bytes 8656384 | tf_op jit(solution)/shard_map/reduce_sum | solution.py:195
  134.8 7.0 %convolution_convert_fusion.4 = bf16[512,3072]{1,0:T(8,128)(2,1)} fusion(bf16[1408,3072]{1,0:T(8,128)(2,1)S(1)} %copy-done.4, s32[512]{0:T(512)S(1)} %eq.274), kind=kOutput, calls=%fused_computation.74 | convolution fusion | flops 4431478784 | bytes 11798528 | tf_op jit(solution)/shard_map/dot_general | solution.py:49
  141.9 5.8 %shard_map.105 = (f32[8,32,3072]{2,1,0:T(8,128)}, f32[8,32,3072]{2,1,0:T(8,128)}) custom-call(s32[1]{0:T(128)} %bitcast.5.ch, bf16[4,8,32,3072]{3,2,1,0:T(8,128)(2,1)} %get-tuple-element.298.ar.al, bf16[4,8,32,3072]{3,2,1,0:T(8,128)(2,1)} %collective-permute-done.12.br.bl, bf16[4,8,32,3072]{3,2,1,0:T(8,128)(2,1)} %get-tuple-element.298.ar.al, ...), custom_call_target="tpu_custom_call" | custom-call | flops 15728640 | bytes 12582912 | tf_op jit(solution)/shard_map/pallas_call | solution.py:98
  148.8 46.1 %fusion.16 = bf16[4096,3072]{1,0:T(8,128)(2,1)} fusion(s32[4096]{0:T(1024)S(1)} %get-tuple-element.358, bf16[1408,3072]{1,0:T(8,128)(2,1)} %pad_maximum_fusion.3, f32[3072]{0:T(1024)S(1)} %convert_element_type.191, f32[1408]{0:T(1024)S(1)} %add_rsqrt_fusion.1), kind=kOutput, calls=%fused_computation.43 | convolution fusion | flops 35469131776 | bytes 33850880 | tf_op jit(solution)/shard_map/dot_general | solution.py:49
  194.9 10.7 %while.26 = (s32[]{:T(128)}, bf16[4096,3072]{1,0:T(8,128)(2,1)}, bf16[512,3072]{1,0:T(8,128)(2,1)}, s32[]{:T(128)}, s32[4096]{0:T(1024)S(1)}, /*index=5*/s32[409...) while((s32[]{:T(128)}, bf16[4096,3072]{1,0:T(8,128)(2,1)}, ...), condition=%wide.region_10.11_spmd, body=%wide.region_7.10_spmd.sunk | while | flops 40015364096 | bytes 194423376 | solution.py:211
  209.1 3.6 slice_add_fusion.3
  212.9 3.1 collective-permute-start.20
  216.0 49.6 %collective-permute-done.15 = f32[8,32,3072]{2,1,0:T(8,128)} collective-permute-done((f32[8,32,3072]{2,1,0:T(8,128)}, f32[8,32,3072]{2,1,0:T(8,128)}, u32[]{:S(2)}, u32[]{:S(2)}) %collective-permute-start.15) | collective-permute-done | bytes 3145760 | tf_op jit(solution)/shard_map/ppermute | solution.py:52
  265.6 12.4 %collective-permute-done.13 = f32[8,32,3072]{2,1,0:T(8,128)S(1)} collective-permute-done((f32[8,32,3072]{2,1,0:T(8,128)}, f32[8,32,3072]{2,1,0:T(8,128)S(1)}, u32[]{:S(2)}, u32[]{:S(2)}) %collective-permute-start.13) | collective-permute-done | bytes 3145760 | tf_op jit(solution)/shard_map/ppermute | solution.py:52
  278.1 3.7 slice_add_fusion.7
  281.7 3.2 collective-permute-start.16
  285.0 46.7 %convolution_convert_fusion.2 = bf16[4096,1536]{1,0:T(8,128)(2,1)} fusion(bf16[4096,3072]{1,0:T(8,128)(2,1)} %get-tuple-element.290, bf16[3072,1536]{1,0:T(8,128)(2,1)} %w_ref.3), kind=kOutput, calls=%fused_computation.49 | convolution fusion | flops 38660997120 | bytes 47185920 | tf_op jit(solution)/shard_map/dot_general | solution.py:49
  332.4 11.1 %collective-permute-done.14 = f32[4,32,3072]{2,1,0:T(8,128)S(1)} collective-permute-done((f32[4,32,3072]{2,1,0:T(8,128)}, f32[4,32,3072]{2,1,0:T(8,128)S(1)}, u32[]{:S(2)}, u32[]{:S(2)}) %collective-permute-start.14) | collective-permute-done | bytes 1572896 | tf_op jit(solution)/shard_map/ppermute | solution.py:52
  343.5 3.7 slice_add_fusion.1
  347.2 2.8 slice_add_fusion.5
  352.4 3.2 fusion.31
  355.6 4.2 convolution_convert_fusion.3
  359.8 5.0 %all-to-all-start.1 = ((bf16[8,96,3072]{2,1,0:T(8,128)(2,1)}), bf16[8,96,3072]{2,1,0:T(8,128)(2,1)}, u32[]{:S(2)}, u32[]{:S(2)}) async-start(bf16[8,96,3072]{2,1,0:T(8,128)(2,1)} %bitcast.94), calls=%async_computation.1 | async-start | bytes 9437184 | tf_op jit(solution)/shard_map/all_to_all | solution.py:242
  364.8 48.6 %fusion.114 = f32[3072,1536]{1,0:T(8,128)} fusion(bf16[4096,3072]{1,0:T(8,128)(2,1)} %get-tuple-element.290, bf16[4096,1536]{1,0:T(8,128)(2,1)} %bitcast.102), kind=kOutput, calls=%fused_computation.247 | convolution fusion | flops 38654705664 | bytes 56623104 | tf_op jit(solution)/shard_map/dot_general | solution.py:49
  413.4 6.6 %all-to-all-done.1 = bf16[8,96,3072]{2,1,0:T(8,128)(2,1)} async-done(((bf16[8,96,3072]{2,1,0:T(8,128)(2,1)}), bf16[8,96,3072]{2,1,0:T(8,128)(2,1)}, u32[]{:S(2)}, u32[]{:S(2)}) %all-to-all-start.1) | async-done | bytes 4718624 | tf_op jit(solution)/shard_map/all_to_all | solution.py:242
  420.6 3.6 all-to-all-start.2
  424.3 15.6 %fusion.34 = f32[2048,3072]{1,0:T(8,128)} fusion(bf16[768,3072]{1,0:T(8,128)(2,1)} %bitcast.27, s32[768]{0:T(1024)S(1)} %copy-done.26), kind=kOutput, calls=%fused_computation.69 | convolution fusion | flops 9665249280 | bytes 29887488 | tf_op jit(solution)/shard_map/dot_general | solution.py:49
  (117 shorter events, 24.4 us)
Async XLA Ops:
  11.9 57.4 %copy-start.8 = (bf16[176,3072]{1,0:T(8,128)(2,1)}, bf16[176,3072]{1,0:T(8,128)(2,1)S(1)}, u32[]{:S(2)}) copy-start(bf16[176,3072]{1,0:T(8,128)(2,1)S(1)} %gather_fusion.1) | copy-start | bytes 3244036
  11.9 27.9 %collective-permute-start.5 = (bf16[176,3072]{1,0:T(8,128)(2,1)S(1)}, bf16[176,3072]{1,0:T(8,128)(2,1)S(1)}, u32[]{:S(2)}, u32[]{:S(2)}) collective-permute-start(bf16[176,3072]{1,0:T(8,128)(2,1)S(1)} %gather_fusion.1), channel_id=1, source_target_pairs={{0,2},{1,3},{2,4},{3,5},{4,6},{5,7},{6,0},{7,1},{8,10},{9,11},{10,... | collective-permute-start | bytes 3244040 | tf_op jit(solution)/shard_map/ppermute | solution.py:52
  14.3 25.8 %collective-permute-start.6 = (bf16[176,3072]{1,0:T(8,128)(2,1)S(1)}, bf16[176,3072]{1,0:T(8,128)(2,1)S(1)}, u32[]{:S(2)}, u32[]{:S(2)}) collective-permute-start(bf16[176,3072]{1,0:T(8,128)(2,1)S(1)} %gather_fusion.1), channel_id=1, source_target_pairs={{0,6},{1,7},{2,0},{3,1},{4,2},{5,3},{6,4},{7,5},{8,14},{9,15},{10,... | collective-permute-start | bytes 3244040 | tf_op jit(solution)/shard_map/ppermute | solution.py:52
  39.8 29.5 %copy-start.10 = (bf16[176,3072]{1,0:T(8,128)(2,1)}, bf16[176,3072]{1,0:T(8,128)(2,1)S(1)}, u32[]{:S(2)}) copy-start(bf16[176,3072]{1,0:T(8,128)(2,1)S(1)} %collective-permute-done.5.x1) | copy-start | bytes 3244036
  39.8 29.5 %collective-permute-start.7 = (bf16[88,3072]{1,0:T(8,128)(2,1)S(1)}, bf16[88,3072]{1,0:T(8,128)(2,1)}, u32[]{:S(2)}, u32[]{:S(2)}) collective-permute-start(bf16[88,3072]{1,0:T(8,128)(2,1)S(1)} %slice.64), channel_id=1, source_target_pairs={{0,2},{1,3},{2,4},{3,5},{4,6},{5,7},{6,0},{7,1},{8,10},{9,11},{10,... | collective-permute-start | bytes 1622024 | tf_op jit(solution)/shard_map/ppermute | solution.py:52
  40.1 29.2 %copy-start.11 = (bf16[176,3072]{1,0:T(8,128)(2,1)}, bf16[176,3072]{1,0:T(8,128)(2,1)S(1)}, u32[]{:S(2)}) copy-start(bf16[176,3072]{1,0:T(8,128)(2,1)S(1)} %collective-permute-done.6.x2) | copy-start | bytes 3244036
  40.2 29.2 %collective-permute-start.8 = (bf16[88,3072]{1,0:T(8,128)(2,1)S(1)}, bf16[88,3072]{1,0:T(8,128)(2,1)}, u32[]{:S(2)}, u32[]{:S(2)}) collective-permute-start(bf16[88,3072]{1,0:T(8,128)(2,1)S(1)} %slice.65), channel_id=1, source_target_pairs={{0,6},{1,7},{2,0},{3,1},{4,2},{5,3},{6,4},{7,5},{8,14},{9,15},{10,... | collective-permute-start | bytes 1622024 | tf_op jit(solution)/shard_map/ppermute | solution.py:52
  69.3 51.9 %collective-permute-start.10 = (bf16[4,8,32,3072]{3,2,1,0:T(8,128)(2,1)}, bf16[4,8,32,3072]{3,2,1,0:T(8,128)(2,1)}, u32[]{:S(2)}, u32[]{:S(2)}) collective-permute-start(bf16[4,8,32,3072]{3,2,1,0:T(8,128)(2,1)} %get-tuple-element.287), channel_id=1, source_target_pairs={{0,1},{1,0},{2,3},{3,2},{4,5},{5,4},{6,7},{7,6},{8,9},{9,8},{10,11... | collective-permute-start | bytes 18874376 | tf_op jit(solution)/shard_map/ppermute | solution.py:52
  73.8 26.1 %copy-start.19 = (s32[16,256]{1,0:T(8,128)S(1)}, s32[16,256]{1,0:T(8,128)}, u32[]{:S(2)}) copy-start(s32[16,256]{1,0:T(8,128)} %param.10) | copy-start | bytes 49156
  73.8 39.6 %collective-permute-start.9 = (bf16[704,3072]{1,0:T(8,128)(2,1)}, bf16[704,3072]{1,0:T(8,128)(2,1)}, u32[]{:S(2)}, u32[]{:S(2)}) collective-permute-start(bf16[704,3072]{1,0:T(8,128)(2,1)} %shard_map.101), channel_id=1, source_target_pairs={{0,1},{1,0},{2,3},{3,2},{4,5},{5,4},{6,7},{7,6},{8,9},{9,8},{10,11... | collective-permute-start | bytes 12976136 | tf_op jit(solution)/shard_map/ppermute | solution.py:52
  99.9 41.9 %collective-permute-start.12 = (bf16[4,8,32,3072]{3,2,1,0:T(8,128)(2,1)}, bf16[4,8,32,3072]{3,2,1,0:T(8,128)(2,1)}, u32[]{:S(2)}, u32[]{:S(2)}) collective-permute-start(bf16[4,8,32,3072]{3,2,1,0:T(8,128)(2,1)} %get-tuple-element.293), channel_id=1, source_target_pairs={{0,1},{1,0},{2,3},{3,2},{4,5},{5,4},{6,7},{7,6},{8,9},{9,8},{10,11... | collective-permute-start | bytes 18874376 | tf_op jit(solution)/shard_map/ppermute | solution.py:52
  100.2 21.0 %copy-start.12 = (s32[8,512]{1,0:T(8,128)}, s32[8,512]{1,0:T(8,128)S(1)}, u32[]{:S(2)}) copy-start(s32[8,512]{1,0:T(8,128)S(1)} %reshape.446) | copy-start | bytes 49156
  109.1 3.7 collective-permute-start.11
  126.9 82.1 %collective-permute-start.19 = (f32[8,32,3072]{2,1,0:T(8,128)}, f32[8,32,3072]{2,1,0:T(8,128)}, u32[]{:S(2)}, u32[]{:S(2)}) collective-permute-start(f32[8,32,3072]{2,1,0:T(8,128)} %get-tuple-element.288), channel_id=1, source_target_pairs={{0,6},{1,7},{2,0},{3,1},{4,2},{5,3},{6,4},{7,5},{8,14},{9,15},{10,... | collective-permute-start | bytes 9437192 | tf_op jit(solution)/shard_map/ppermute | solution.py:52
  127.5 81.6 %collective-permute-start.17 = (f32[8,32,3072]{2,1,0:T(8,128)}, f32[8,32,3072]{2,1,0:T(8,128)}, u32[]{:S(2)}, u32[]{:S(2)}) collective-permute-start(f32[8,32,3072]{2,1,0:T(8,128)} %get-tuple-element.302), channel_id=1, source_target_pairs={{0,2},{1,3},{2,4},{3,5},{4,6},{5,7},{6,0},{7,1},{8,10},{9,11},{10,... | collective-permute-start | bytes 9437192 | tf_op jit(solution)/shard_map/ppermute | solution.py:52
  147.7 118.0 %collective-permute-start.15 = (f32[8,32,3072]{2,1,0:T(8,128)}, f32[8,32,3072]{2,1,0:T(8,128)}, u32[]{:S(2)}, u32[]{:S(2)}) collective-permute-start(f32[8,32,3072]{2,1,0:T(8,128)} %get-tuple-element.297), channel_id=1, source_target_pairs={{0,6},{1,7},{2,0},{3,1},{4,2},{5,3},{6,4},{7,5},{8,14},{9,15},{10,... | collective-permute-start | bytes 9437192 | tf_op jit(solution)/shard_map/ppermute | solution.py:52
  194.9 11.7 %copy-start.24 = (pred[8,512]{1,0:T(8,128)(4,1)S(1)}, pred[8,512]{1,0:T(8,128)(4,1)}, u32[]{:S(2)}) copy-start(pred[8,512]{1,0:T(8,128)(4,1)} %get-tuple-element.351) | copy-start | bytes 12292
  205.6 72.5 %collective-permute-start.13 = (f32[8,32,3072]{2,1,0:T(8,128)}, f32[8,32,3072]{2,1,0:T(8,128)S(1)}, u32[]{:S(2)}, u32[]{:S(2)}) collective-permute-start(f32[8,32,3072]{2,1,0:T(8,128)} %get-tuple-element.296), channel_id=1, source_target_pairs={{0,2},{1,3},{2,4},{3,5},{4,6},{5,7},{6,0},{7,1},{8,10},{9,11},{10,... | collective-permute-start | bytes 9437192 | tf_op jit(solution)/shard_map/ppermute | solution.py:52
  209.1 69.0 %copy-start.3 = (bf16[4,8,32,3072]{3,2,1,0:T(8,128)(2,1)S(1)}, bf16[4,8,32,3072]{3,2,1,0:T(8,128)(2,1)}, u32[]{:S(2)}) copy-start(bf16[4,8,32,3072]{3,2,1,0:T(8,128)(2,1)} %get-tuple-element.298.ar.al) | copy-start | bytes 18874372
  212.7 119.7 %collective-permute-start.18 = (f32[4,32,3072]{2,1,0:T(8,128)S(1)}, f32[4,32,3072]{2,1,0:T(8,128)S(1)}, u32[]{:S(2)}, u32[]{:S(2)}) collective-permute-start(f32[4,32,3072]{2,1,0:T(8,128)S(1)} %get-tuple-element.368), channel_id=1, source_target_pairs={{0,2},{1,3},{2,4},{3,5},{4,6},{5,7},{6,0},{7,1},{8,10},{9,11},{10,... | collective-permute-start | bytes 4718600 | tf_op jit(solution)/shard_map/ppermute | solution.py:52
  212.9 119.5 %collective-permute-start.20 = (f32[4,32,3072]{2,1,0:T(8,128)S(1)}, f32[4,32,3072]{2,1,0:T(8,128)S(1)}, u32[]{:S(2)}, u32[]{:S(2)}) collective-permute-start(f32[4,32,3072]{2,1,0:T(8,128)S(1)} %get-tuple-element.369), channel_id=1, source_target_pairs={{0,6},{1,7},{2,0},{3,1},{4,2},{5,3},{6,4},{7,5},{8,14},{9,15},{10,... | collective-permute-start | bytes 4718600 | tf_op jit(solution)/shard_map/ppermute | solution.py:52
  281.7 61.7 %collective-permute-start.14 = (f32[4,32,3072]{2,1,0:T(8,128)}, f32[4,32,3072]{2,1,0:T(8,128)S(1)}, u32[]{:S(2)}, u32[]{:S(2)}) collective-permute-start(f32[4,32,3072]{2,1,0:T(8,128)} %get-tuple-element.364), channel_id=1, source_target_pairs={{0,2},{1,3},{2,4},{3,5},{4,6},{5,7},{6,0},{7,1},{8,10},{9,11},{10,... | collective-permute-start | bytes 4718600 | tf_op jit(solution)/shard_map/ppermute | solution.py:52
  281.7 49.9 %copy-start.7 = (bf16[512,3072]{1,0:T(8,128)(2,1)S(1)}, bf16[512,3072]{1,0:T(8,128)(2,1)}, u32[]{:S(2)}) copy-start(bf16[512,3072]{1,0:T(8,128)(2,1)} %get-tuple-element.291) | copy-start | bytes 9437188
  281.7 61.7 %collective-permute-start.16 = (f32[4,32,3072]{2,1,0:T(8,128)S(1)}, f32[4,32,3072]{2,1,0:T(8,128)S(1)}, u32[]{:S(2)}, u32[]{:S(2)}) collective-permute-start(f32[4,32,3072]{2,1,0:T(8,128)S(1)} %get-tuple-element.365), channel_id=1, source_target_pairs={{0,6},{1,7},{2,0},{3,1},{4,2},{5,3},{6,4},{7,5},{8,14},{9,15},{10,... | collective-permute-start | bytes 4718600 | tf_op jit(solution)/shard_map/ppermute | solution.py:52
  359.8 60.2 %all-to-all-start.1 = ((bf16[8,96,3072]{2,1,0:T(8,128)(2,1)}), bf16[8,96,3072]{2,1,0:T(8,128)(2,1)}, u32[]{:S(2)}, u32[]{:S(2)}) async-start(bf16[8,96,3072]{2,1,0:T(8,128)(2,1)} %bitcast.94), calls=%async_computation.1 | async-start | bytes 9437184 | tf_op jit(solution)/shard_map/all_to_all | solution.py:242
  364.8 59.4 %copy-start.26 = (s32[768]{0:T(1024)S(1)}, s32[768]{0:T(1024)}, u32[]{:S(2)}) copy-start(s32[768]{0:T(1024)} %sub.177) | copy-start | bytes 9220
  420.6 19.2 %all-to-all-start.2 = ((f32[8,1,3072]{2,1,0:T(1,128)}), f32[8,1,3072]{2,1,0:T(1,128)S(1)}, u32[]{:S(2)}, u32[]{:S(2)}) async-start(f32[8,1,3072]{2,1,0:T(1,128)} %broadcast_in_dim.108), calls=%async_computation.2 | async-start | bytes 196608 | tf_op jit(solution)/shard_map/all_to_all | solution.py:253
  424.2 16.3 %copy-start.14 = (s32[8,512]{1,0:T(8,128)S(1)}, s32[8,512]{1,0:T(8,128)}, u32[]{:S(2)}) copy-start(s32[8,512]{1,0:T(8,128)} %copy-done.12) | copy-start | bytes 49156
  424.2 16.3 %copy-start.16 = (s32[8,512]{1,0:T(8,128)S(1)}, s32[8,512]{1,0:T(8,128)}, u32[]{:S(2)}) copy-start(s32[8,512]{1,0:T(8,128)} %copy-done.15) | copy-start | bytes 49156
  424.2 16.3 %copy-start.18 = (s32[8,512]{1,0:T(8,128)S(1)}, s32[8,512]{1,0:T(8,128)}, u32[]{:S(2)}) copy-start(s32[8,512]{1,0:T(8,128)} %copy-done.17) | copy-start | bytes 49156
  424.3 16.3 %copy-start.20 = (s32[1,512]{1,0:T(1,128)S(1)}, s32[1,512]{1,0:T(1,128)}, u32[]{:S(2)}) copy-start(s32[1,512]{1,0:T(1,128)} %get-tuple-element.354) | copy-start | bytes 6148
  424.3 16.3 %copy-start.21 = (s32[1,512]{1,0:T(1,128)S(1)}, s32[1,512]{1,0:T(1,128)}, u32[]{:S(2)}) copy-start(s32[1,512]{1,0:T(1,128)} %get-tuple-element.355) | copy-start | bytes 6148
  (8 other events, 60.2 us)

commit v2 on v1

--- a/solution.py
+++ b/solution.py
@@ -34,6 +34,26 @@
     for x in (x0, x1, x2, x3, x4):
         o_ref[at:at + x.shape[0], :] = x[...]
         at += x.shape[0]
+
+
+def dx_kernel(ch, keep, got, ra, la, rb, lb, x_ref, dres, g_ref, *rest):
+    dx_ref, dg_ref = rest[-2:]
+    f32 = jnp.float32
+    k = pl.program_id(0)
+    far = jnp.where(k < pl.num_programs(0) // 2, ra[...] + la[...], rb[...] + lb[...])
+    dn = keep[0].astype(f32) + got[0].astype(f32) + far
+    x = x_ref[...].astype(f32)
+    rs = lax.rsqrt(jnp.mean(x * x, axis=-1, keepdims=True) + EPS)
+    nh = x * rs
+    gdn = g_ref[...] * dn
+    dx = dres[...].astype(f32) + rs * (gdn - nh * jnp.mean(nh * gdn, axis=-1, keepdims=True))
+    dx_ref[...] = dx.astype(jnp.bfloat16)
+
+    @pl.when(k == 0)
+    def _():
+        dg_ref[...] = jnp.zeros_like(dg_ref)
+
+    dg_ref[...] += jnp.sum(jnp.sum(dn * nh, axis=0), axis=0, keepdims=True)
 
 
 def solution(mesh):
@@ -214,22 +234,37 @@
             after(c, n)
             pass_on(c, ch)
         u = mm(n, W)
+        dxb, dgs = None, []
         for c in range(nc):
             after(c, (relay[c], u))
-        dns = []
-        for c in range(nc):
-            kc, ka = sizes[c], sizes[c] // 2
-            dns.append(term(c, ch, 0, ka) + relay[c][0] + near[c][1][:ka])
-            dns.append(term(c, ch, ka, kc) + near[c][0][ka:] + relay[c][1])
-        dn = jnp.concatenate(dns, axis=0).reshape(nl, d)
-
-        xf = xl.astype(f32)
-        rs = lax.rsqrt(jnp.mean(xf * xf, axis=-1, keepdims=True) + EPS)
-        nh = xf * rs
-        gdn = gf * dn
-        dx = dres.reshape(nl, d).astype(f32) + rs * (gdn - nh * jnp.mean(nh * gdn, axis=-1, keepdims=True))
-        dxb = dx.astype(bf16)
-        dgp = jnp.sum(dn * nh, axis=0)
+            kc, kb = sizes[c], 1
+            na = kc // 2 // kb
+            k0 = starts[c] // kb
+            part = (kb, ts, d)
+            mine = pl.BlockSpec((1,) + part, lambda k, s: (s[0], k, 0, 0))
+            low = pl.BlockSpec(part, lambda k, s, na=na: (jnp.minimum(k, na - 1), 0, 0))
+            high = pl.BlockSpec(part, lambda k, s, na=na: (jnp.maximum(k, na), 0, 0))
+            high0 = pl.BlockSpec(part, lambda k, s, na=na: (jnp.maximum(k - na, 0), 0, 0))
+            tok = pl.BlockSpec(part, lambda k, s, k0=k0: (k0 + k, 0, 0))
+            row = pl.BlockSpec((1, d), lambda k, s: (0, 0))
+            ins = [ps[c], gots[c], relay[c][0], near[c][1], near[c][0], relay[c][1], xl.reshape(nk, ts, d), dres, gf.reshape(1, d)]
+            specs = [mine, mine, low, low, high, high0, tok, tok, row]
+            alias = {}
+            if dxb is not None:
+                ins.append(dxb)
+                specs.append(pl.BlockSpec(memory_space=pl.ANY))
+                alias = {len(ins): 0}
+            dxb, dgc = pl.pallas_call(
+                dx_kernel,
+                grid_spec=pltpu.PrefetchScalarGridSpec(num_scalar_prefetch=1, grid=(kc // kb,), in_specs=specs, out_specs=[tok, row]),
+                out_shape=[jax.ShapeDtypeStruct((nk, ts, d), bf16), jax.ShapeDtypeStruct((1, d), f32)],
+                input_output_aliases=alias,
+                compiler_params=pltpu.CompilerParams(vmem_limit_bytes=40 * 1024 * 1024),
+                cost_estimate=pl.CostEstimate(flops=40 * kc * ts * d, bytes_accessed=18 * kc * ts * d, transcendentals=0),
+            )(ch.reshape(1), *ins)
+            dgs.append(dgc)
+        dxb = dxb.reshape(nl, d)
+        dgp = sum(dgs[1:], dgs[0])[0]
 
         ownm = lax.dynamic_index_in_dim(ownh, me, 0, keepdims=False)
         rankm = lax.dynamic_index_in_dim(rank, me, 0, keepdims=False)

time: 447 us -> 463 us (1.036)
  Pallas kernels: 67.6 us -> 83.4 us
  other arithmetic: 38.6 us -> 24.5 us
  waiting for transfers between devices: 105 us -> 118 us
    pallas_call x0 -> x2, Pallas kernels: none -> 15.7 us  [work(): pl.pallas_call(dx_kernel, grid_spec=pltpu.PrefetchScalarGridSpec(num_scal...]
    ppermute x16, waiting for transfers between devices: 98.3 us -> 111 us  [send(): return lax.ppermute(a, axis, ring)]
    add x4 -> x3, other arithmetic: 13.8 us -> 6.44 us  [the longest x2 6.43 us: pass_on(): qb = term(c, chip + nch - 1, ka, kc) + near[c][1][ka:]]
  transfers between devices with their start and end apart: 18 -> 18, of which waited for: 6 -> 6; matrix products, arithmetic and copies ran while one was open for 44% -> 42% of each run, Pallas kernels for 15% -> 15%
where the time goes in v2:
time: 463 us; the launch traced here: 457 us
  matrix products  174 us (38%)
  waiting for transfers between devices  118 us (25%)
  Pallas kernels  83.4 us (18%)
  starting transfers between devices  29.1 us (6%)
  other arithmetic  24.5 us (5%)
  local copies, waits for them, and re-layouts  12.8 us (3%)
  loops' own time  8.39 us (2%)
  between operations  6.24 us (1%)
    dot_general x12, matrix products, dot(): return lax.dot_general(a, b, dims, preferred_element_type=f32)  174 us
    ppermute x16, waiting for transfers between devices, send(): return lax.ppermute(a, axis, ring)  111 us
    pallas_call x2, Pallas kernels, work(): pl.pallas_call(terms_kernel, grid_spec=pltpu.PrefetchScalarGridSpec(num_s...  51.7 us
    ppermute x16, starting transfers between devices, send(): return lax.ppermute(a, axis, ring)  20.6 us
    pallas_call x2, Pallas kernels, work(): pl.pallas_call(dx_kernel, grid_spec=pltpu.PrefetchScalarGridSpec(num_scal...  15.7 us
    pallas_call x2, Pallas kernels, spread(): pl.pallas_call(spread_kernel, grid_spec=pltpu.PrefetchScalarGridSpec(num_...  11.6 us
  transfers between devices with their start and end apart: 18, of which 6 were waited for; matrix products, arithmetic and copies ran while one was open for 42% of the time, Pallas kernels for 15%

profile of v2, /device:TPU:112, one launch (start us, length us, event | category | flops | bytes accessed | tf_op | source)
XLA Modules:
  0.0 456.6 jit_solution(13417964330866053329)
XLA Ops:
  3.3 8.5 %gather_fusion.1 = bf16[176,3072]{1,0:T(8,128)(2,1)S(1)} fusion(bf16[2048,3072]{1,0:T(8,128)(2,1)} %param.11, s32[1024]{0:T(1024)S(1)} %pad_clamp_fusion.1), kind=kCustom, calls=%fused_computation.1 | custom fusion | bytes 2163392 | tf_op jit(solution)/shard_map/jit(_take)/gather | solution.py:203
  11.9 4.0 collective-permute-start.6
  15.9 23.2 %collective-permute-done.6.x2 = bf16[176,3072]{1,0:T(8,128)(2,1)S(1)} collective-permute-done((bf16[176,3072]{1,0:T(8,128)(2,1)S(1)}, bf16[176,3072]{1,0:T(8,128)(2,1)S(1)}, u32[]{:S(2)}, u32[]{:S(2)}) %collective-permute-start.6) | collective-permute-done | bytes 1081376 | tf_op jit(solution)/shard_map/ppermute | solution.py:72
  39.1 3.8 collective-permute-start.8
  43.0 26.1 %shard_map.102 = (bf16[4,8,32,3072]{3,2,1,0:T(8,128)(2,1)}, bf16[4,8,32,3072]{3,2,1,0:T(8,128)(2,1)}) custom-call(s32[1]{0:T(128)} %bitcast.6.co, bf16[16,256,1536]{2,1,0:T(8,128)(2,1)} %a_ref.3, bf16[3072,1536]{1,0:T(8,128)(2,1)} %w_ref.3), custom_call_target="tpu_custom_call" | custom-call | flops 19327352832 | bytes 25165824 | tf_op jit(solution)/shard_map/pallas_call | solution.py:133
  69.2 4.5 shard_map.101
  74.2 25.6 %shard_map.104 = (bf16[4,8,32,3072]{3,2,1,0:T(8,128)(2,1)}, bf16[4,8,32,3072]{3,2,1,0:T(8,128)(2,1)}) custom-call(s32[1]{0:T(128)} %bitcast.6.co, bf16[16,256,1536]{2,1,0:T(8,128)(2,1)} %a_ref.3, bf16[3072,1536]{1,0:T(8,128)(2,1)} %w_ref.3), custom_call_target="tpu_custom_call" | custom-call | flops 19327352832 | bytes 25165824 | tf_op jit(solution)/shard_map/pallas_call | solution.py:133
  109.0 2.1 collective-permute-start.11
  113.4 7.8 %pad_maximum_fusion.3 = bf16[1408,3072]{1,0:T(8,128)(2,1)} fusion(bf16[704,3072]{1,0:T(8,128)(2,1)} %collective-permute-done.9, bf16[704,3072]{1,0:T(8,128)(2,1)} %shard_map.101), kind=kLoop, calls=%fused_computation.51 | loop fusion | flops 17301504 | bytes 17301504 | tf_op jit(solution)/shard_map/concatenate | solution.py:211
  121.1 5.8 %shard_map.103 = (f32[8,32,3072]{2,1,0:T(8,128)}, f32[8,32,3072]{2,1,0:T(8,128)}) custom-call(s32[1]{0:T(128)} %bitcast.5.ch, bf16[4,8,32,3072]{3,2,1,0:T(8,128)(2,1)} %get-tuple-element.299.ar.al.keep, bf16[4,8,32,3072]{3,2,1,0:T(8,128)(2,1)} %collective-permute-done.10.br.bl.got, bf16[4,8,32,3072]{3,2,1,0:T(8,128)(2,1)} %get-tuple-element.299.ar.al.keep, ...), custom_call_target="tpu_custom_call" | custom-call | flops 15728640 | bytes 12582912 | tf_op jit(solution)/shard_map/pallas_call | solution.py:118
  127.0 5.4 %fusion.17 = f32[1408]{0:T(1024)S(1)} fusion(bf16[1408,3072]{1,0:T(8,128)(2,1)} %pad_maximum_fusion.3), kind=kLoop, calls=%fused_computation.46 | loop fusion | flops 12974720 | bytes 8656384 | tf_op jit(solution)/shard_map/reduce_sum | solution.py:215
  132.9 7.0 %convolution_convert_fusion.4 = bf16[512,3072]{1,0:T(8,128)(2,1)} fusion(bf16[1408,3072]{1,0:T(8,128)(2,1)S(1)} %copy-done.4, s32[512]{0:T(512)S(1)} %eq.266), kind=kOutput, calls=%fused_computation.60 | convolution fusion | flops 4431478784 | bytes 11798528 | tf_op jit(solution)/shard_map/dot_general | solution.py:69
  139.9 5.8 %shard_map.105 = (f32[8,32,3072]{2,1,0:T(8,128)}, f32[8,32,3072]{2,1,0:T(8,128)}) custom-call(s32[1]{0:T(128)} %bitcast.5.ch, bf16[4,8,32,3072]{3,2,1,0:T(8,128)(2,1)} %get-tuple-element.307.ar.al.keep, bf16[4,8,32,3072]{3,2,1,0:T(8,128)(2,1)} %collective-permute-done.16.br.bl.got, bf16[4,8,32,3072]{3,2,1,0:T(8,128)(2,1)} %get-tuple-element.307.ar.al.keep, ...), custom_call_target="tpu_custom_call" | custom-call | flops 15728640 | bytes 12582912 | tf_op jit(solution)/shard_map/pallas_call | solution.py:118
  146.7 2.2 collective-permute-start.19
  148.9 46.1 %fusion.16 = bf16[4096,3072]{1,0:T(8,128)(2,1)} fusion(s32[4096]{0:T(1024)S(1)} %get-tuple-element.364, bf16[1408,3072]{1,0:T(8,128)(2,1)} %pad_maximum_fusion.3, f32[3072]{0:T(1024)S(1)} %convert_element_type.147, f32[1408]{0:T(1024)S(1)} %add_rsqrt_fusion.1), kind=kOutput, calls=%fused_computation.43 | convolution fusion | flops 35469131776 | bytes 33850880 | tf_op jit(solution)/shard_map/dot_general | solution.py:69
  195.0 7.5 %while.26 = (s32[]{:T(128)}, bf16[4096,3072]{1,0:T(8,128)(2,1)}, bf16[512,3072]{1,0:T(8,128)(2,1)}, s32[]{:T(128)}, s32[4096]{0:T(1024)S(1)}, /*index=5*/s32[409...) while((s32[]{:T(128)}, bf16[4096,3072]{1,0:T(8,128)(2,1)}, ...), condition=%wide.region_10.11_spmd, body=%wide.region_7.10_spmd.sunk | while | flops 40015364096 | bytes 194423376 | solution.py:231
  202.6 2.0 collective-permute-start.14
  207.1 58.7 %collective-permute-done.17.rb = f32[8,32,3072]{2,1,0:T(8,128)} collective-permute-done((f32[8,32,3072]{2,1,0:T(8,128)}, f32[8,32,3072]{2,1,0:T(8,128)}, u32[]{:S(2)}, u32[]{:S(2)}) %collective-permute-start.17) | collective-permute-done | bytes 3145760 | tf_op jit(solution)/shard_map/ppermute | solution.py:72
  265.7 3.5 slice_add_fusion
  271.3 14.8 %collective-permute-done.14.la = f32[8,32,3072]{2,1,0:T(8,128)S(1)} collective-permute-done((f32[8,32,3072]{2,1,0:T(8,128)}, f32[8,32,3072]{2,1,0:T(8,128)S(1)}, u32[]{:S(2)}, u32[]{:S(2)}) %collective-permute-start.14) | collective-permute-done | bytes 3145760 | tf_op jit(solution)/shard_map/ppermute | solution.py:72
  286.1 3.0 slice_add_fusion.2
  289.1 2.6 collective-permute-start.15
  291.8 46.9 %convolution_convert_fusion.2 = bf16[4096,1536]{1,0:T(8,128)(2,1)} fusion(bf16[4096,3072]{1,0:T(8,128)(2,1)} %get-tuple-element.294, bf16[3072,1536]{1,0:T(8,128)(2,1)} %w_ref.3), kind=kOutput, calls=%fused_computation.49 | convolution fusion | flops 38660997120 | bytes 47185920 | tf_op jit(solution)/shard_map/dot_general | solution.py:69
  338.6 13.3 %collective-permute-done.15.lb = f32[4,32,3072]{2,1,0:T(8,128)S(1)} collective-permute-done((f32[4,32,3072]{2,1,0:T(8,128)S(1)}, f32[4,32,3072]{2,1,0:T(8,128)S(1)}, u32[]{:S(2)}, u32[]{:S(2)}) %collective-permute-start.15) | collective-permute-done | bytes 1572896 | tf_op jit(solution)/shard_map/ppermute | solution.py:72
  351.9 8.0 %shard_map.106 = (bf16[16,32,3072]{2,1,0:T(8,128)(2,1)}, f32[1,3072]{1,0:T(1,128)S(1)}) custom-call(s32[1]{0:T(128)} %bitcast.5.ch, bf16[4,8,32,3072]{3,2,1,0:T(8,128)(2,1)} %get-tuple-element.307.ar.al.keep, bf16[4,8,32,3072]{3,2,1,0:T(8,128)(2,1)} %collective-permute-done.16.br.bl.got, f32[4,32,3072]{2,1,0:T(8,128)S(1)} %collective-permute-done.18.ra, ...), custom_call_target="tpu_custom_call" | custom-call | flops 31457280 | bytes 14155776 | tf_op jit(solution)/shard_map/pallas_call | solution.py:257
  359.9 7.7 %shard_map.107 = (bf16[16,32,3072]{2,1,0:T(8,128)(2,1)}, f32[1,3072]{1,0:T(1,128)S(1)}) custom-call(s32[1]{0:T(128)} %bitcast.5.ch, bf16[4,8,32,3072]{3,2,1,0:T(8,128)(2,1)} %get-tuple-element.299.ar.al.keep, bf16[4,8,32,3072]{3,2,1,0:T(8,128)(2,1)} %collective-permute-done.10.br.bl.got, ...), custom_call_target="tpu_custom_call", output_to_operand_aliasing={{0}: (10, {})} | custom-call | flops 31457280 | bytes 14155776 | tf_op jit(solution)/shard_map/pallas_call | solution.py:257
  367.6 6.0 %convolution_convert_fusion.3 = bf16[768,3072]{1,0:T(8,128)(2,1)} fusion(bf16[512,3072]{1,0:T(8,128)(2,1)} %bitcast.78, s32[512]{0:T(512)S(1)} %bitcast.89), kind=kOutput, calls=%fused_computation.56 | convolution fusion | flops 2418671616 | bytes 7866368 | tf_op jit(solution)/shard_map/dot_general | solution.py:69
  373.6 5.0 %all-to-all-start.1 = ((bf16[8,96,3072]{2,1,0:T(8,128)(2,1)}), bf16[8,96,3072]{2,1,0:T(8,128)(2,1)}, u32[]{:S(2)}, u32[]{:S(2)}) async-start(bf16[8,96,3072]{2,1,0:T(8,128)(2,1)} %bitcast.77), calls=%async_computation.1 | async-start | bytes 9437184 | tf_op jit(solution)/shard_map/all_to_all | solution.py:277
  378.6 48.6 %fusion.102 = f32[3072,1536]{1,0:T(8,128)} fusion(bf16[4096,3072]{1,0:T(8,128)(2,1)} %get-tuple-element.294, bf16[4096,1536]{1,0:T(8,128)(2,1)} %bitcast.90), kind=kOutput, calls=%fused_computation.223 | convolution fusion | flops 38654705664 | bytes 56623104 | tf_op jit(solution)/shard_map/dot_general | solution.py:69
  427.2 6.5 %all-to-all-done.1 = bf16[8,96,3072]{2,1,0:T(8,128)(2,1)} async-done(((bf16[8,96,3072]{2,1,0:T(8,128)(2,1)}), bf16[8,96,3072]{2,1,0:T(8,128)(2,1)}, u32[]{:S(2)}, u32[]{:S(2)}) %all-to-all-start.1) | async-done | bytes 4718624 | tf_op jit(solution)/shard_map/all_to_all | solution.py:277
  434.5 3.6 all-to-all-start.2
  438.1 15.7 %fusion.24 = f32[2048,3072]{1,0:T(8,128)} fusion(bf16[768,3072]{1,0:T(8,128)(2,1)} %bitcast.23, s32[768]{0:T(1024)S(1)} %copy-done.26), kind=kOutput, calls=%fused_computation.55 | convolution fusion | flops 9665249280 | bytes 29887488 | tf_op jit(solution)/shard_map/dot_general | solution.py:69
  (112 shorter events, 19.2 us)
Async XLA Ops:
  11.9 57.2 %copy-start.8 = (bf16[176,3072]{1,0:T(8,128)(2,1)}, bf16[176,3072]{1,0:T(8,128)(2,1)S(1)}, u32[]{:S(2)}) copy-start(bf16[176,3072]{1,0:T(8,128)(2,1)S(1)} %gather_fusion.1) | copy-start | bytes 3244036
  11.9 27.2 %collective-permute-start.6 = (bf16[176,3072]{1,0:T(8,128)(2,1)S(1)}, bf16[176,3072]{1,0:T(8,128)(2,1)S(1)}, u32[]{:S(2)}, u32[]{:S(2)}) collective-permute-start(bf16[176,3072]{1,0:T(8,128)(2,1)S(1)} %gather_fusion.1), channel_id=1, source_target_pairs={{0,6},{1,7},{2,0},{3,1},{4,2},{5,3},{6,4},{7,5},{8,14},{9,15},{10,... | collective-permute-start | bytes 3244040 | tf_op jit(solution)/shard_map/ppermute | solution.py:72
  15.9 27.0 %collective-permute-start.5 = (bf16[176,3072]{1,0:T(8,128)(2,1)S(1)}, bf16[176,3072]{1,0:T(8,128)(2,1)S(1)}, u32[]{:S(2)}, u32[]{:S(2)}) collective-permute-start(bf16[176,3072]{1,0:T(8,128)(2,1)S(1)} %gather_fusion.1), channel_id=1, source_target_pairs={{0,2},{1,3},{2,4},{3,5},{4,6},{5,7},{6,0},{7,1},{8,10},{9,11},{10,... | collective-permute-start | bytes 3244040 | tf_op jit(solution)/shard_map/ppermute | solution.py:72
  39.0 30.0 %copy-start.10 = (bf16[176,3072]{1,0:T(8,128)(2,1)}, bf16[176,3072]{1,0:T(8,128)(2,1)S(1)}, u32[]{:S(2)}) copy-start(bf16[176,3072]{1,0:T(8,128)(2,1)S(1)} %collective-permute-done.6.x2) | copy-start | bytes 3244036
  39.1 30.1 %collective-permute-start.8 = (bf16[88,3072]{1,0:T(8,128)(2,1)S(1)}, bf16[88,3072]{1,0:T(8,128)(2,1)}, u32[]{:S(2)}, u32[]{:S(2)}) collective-permute-start(bf16[88,3072]{1,0:T(8,128)(2,1)S(1)} %slice.49), channel_id=1, source_target_pairs={{0,6},{1,7},{2,0},{3,1},{4,2},{5,3},{6,4},{7,5},{8,14},{9,15},{10,... | collective-permute-start | bytes 1622024 | tf_op jit(solution)/shard_map/ppermute | solution.py:72
  42.9 26.2 %copy-start.11 = (bf16[176,3072]{1,0:T(8,128)(2,1)}, bf16[176,3072]{1,0:T(8,128)(2,1)S(1)}, u32[]{:S(2)}) copy-start(bf16[176,3072]{1,0:T(8,128)(2,1)S(1)} %collective-permute-done.5.x1) | copy-start | bytes 3244036
  42.9 26.3 %collective-permute-start.7 = (bf16[88,3072]{1,0:T(8,128)(2,1)S(1)}, bf16[88,3072]{1,0:T(8,128)(2,1)}, u32[]{:S(2)}, u32[]{:S(2)}) collective-permute-start(bf16[88,3072]{1,0:T(8,128)(2,1)S(1)} %slice.48), channel_id=1, source_target_pairs={{0,2},{1,3},{2,4},{3,5},{4,6},{5,7},{6,0},{7,1},{8,10},{9,11},{10,... | collective-permute-start | bytes 1622024 | tf_op jit(solution)/shard_map/ppermute | solution.py:72
  69.1 52.0 %collective-permute-start.10 = (bf16[4,8,32,3072]{3,2,1,0:T(8,128)(2,1)}, bf16[4,8,32,3072]{3,2,1,0:T(8,128)(2,1)}, u32[]{:S(2)}, u32[]{:S(2)}) collective-permute-start(bf16[4,8,32,3072]{3,2,1,0:T(8,128)(2,1)} %get-tuple-element.291), channel_id=1, source_target_pairs={{0,1},{1,0},{2,3},{3,2},{4,5},{5,4},{6,7},{7,6},{8,9},{9,8},{10,11... | collective-permute-start | bytes 18874376 | tf_op jit(solution)/shard_map/ppermute | solution.py:72
  73.7 26.1 %copy-start.19 = (s32[16,256]{1,0:T(8,128)S(1)}, s32[16,256]{1,0:T(8,128)}, u32[]{:S(2)}) copy-start(s32[16,256]{1,0:T(8,128)} %param.10) | copy-start | bytes 49156
  73.7 39.6 %collective-permute-start.9 = (bf16[704,3072]{1,0:T(8,128)(2,1)}, bf16[704,3072]{1,0:T(8,128)(2,1)}, u32[]{:S(2)}, u32[]{:S(2)}) collective-permute-start(bf16[704,3072]{1,0:T(8,128)(2,1)} %shard_map.101), channel_id=1, source_target_pairs={{0,1},{1,0},{2,3},{3,2},{4,5},{5,4},{6,7},{7,6},{8,9},{9,8},{10,11... | collective-permute-start | bytes 12976136 | tf_op jit(solution)/shard_map/ppermute | solution.py:72
  99.8 40.1 %collective-permute-start.16 = (bf16[4,8,32,3072]{3,2,1,0:T(8,128)(2,1)}, bf16[4,8,32,3072]{3,2,1,0:T(8,128)(2,1)}, u32[]{:S(2)}, u32[]{:S(2)}) collective-permute-start(bf16[4,8,32,3072]{3,2,1,0:T(8,128)(2,1)} %get-tuple-element.302), channel_id=1, source_target_pairs={{0,1},{1,0},{2,3},{3,2},{4,5},{5,4},{6,7},{7,6},{8,9},{9,8},{10,11... | collective-permute-start | bytes 18874376 | tf_op jit(solution)/shard_map/ppermute | solution.py:72
  100.1 21.0 %copy-start.12 = (s32[8,512]{1,0:T(8,128)}, s32[8,512]{1,0:T(8,128)S(1)}, u32[]{:S(2)}) copy-start(s32[8,512]{1,0:T(8,128)S(1)} %reshape.417) | copy-start | bytes 49156
  109.0 3.7 collective-permute-start.11
  126.9 144.4 %collective-permute-start.12 = (f32[8,32,3072]{2,1,0:T(8,128)}, f32[8,32,3072]{2,1,0:T(8,128)}, u32[]{:S(2)}, u32[]{:S(2)}) collective-permute-start(f32[8,32,3072]{2,1,0:T(8,128)} %get-tuple-element.298), channel_id=1, source_target_pairs={{0,2},{1,3},{2,4},{3,5},{4,6},{5,7},{6,0},{7,1},{8,10},{9,11},{10,... | collective-permute-start | bytes 9437192 | tf_op jit(solution)/shard_map/ppermute | solution.py:72
  145.6 120.1 %collective-permute-start.17 = (f32[8,32,3072]{2,1,0:T(8,128)}, f32[8,32,3072]{2,1,0:T(8,128)}, u32[]{:S(2)}, u32[]{:S(2)}) collective-permute-start(f32[8,32,3072]{2,1,0:T(8,128)} %get-tuple-element.305), channel_id=1, source_target_pairs={{0,2},{1,3},{2,4},{3,5},{4,6},{5,7},{6,0},{7,1},{8,10},{9,11},{10,... | collective-permute-start | bytes 9437192 | tf_op jit(solution)/shard_map/ppermute | solution.py:72
  146.7 119.1 %collective-permute-start.19 = (f32[8,32,3072]{2,1,0:T(8,128)}, f32[8,32,3072]{2,1,0:T(8,128)}, u32[]{:S(2)}, u32[]{:S(2)}) collective-permute-start(f32[8,32,3072]{2,1,0:T(8,128)} %get-tuple-element.306), channel_id=1, source_target_pairs={{0,6},{1,7},{2,0},{3,1},{4,2},{5,3},{6,4},{7,5},{8,14},{9,15},{10,... | collective-permute-start | bytes 9437192 | tf_op jit(solution)/shard_map/ppermute | solution.py:72
  202.6 83.6 %collective-permute-start.14 = (f32[8,32,3072]{2,1,0:T(8,128)}, f32[8,32,3072]{2,1,0:T(8,128)S(1)}, u32[]{:S(2)}, u32[]{:S(2)}) collective-permute-start(f32[8,32,3072]{2,1,0:T(8,128)} %get-tuple-element.292), channel_id=1, source_target_pairs={{0,6},{1,7},{2,0},{3,1},{4,2},{5,3},{6,4},{7,5},{8,14},{9,15},{10,... | collective-permute-start | bytes 9437192 | tf_op jit(solution)/shard_map/ppermute | solution.py:72
  204.6 64.6 %copy-start.15 = (s32[8,512]{1,0:T(8,128)}, s32[8,512]{1,0:T(8,128)S(1)}, u32[]{:S(2)}) copy-start(s32[8,512]{1,0:T(8,128)S(1)} %convert_element_type.154) | copy-start | bytes 49156
  269.2 69.4 %collective-permute-start.20 = (f32[4,32,3072]{2,1,0:T(8,128)S(1)}, f32[4,32,3072]{2,1,0:T(8,128)S(1)}, u32[]{:S(2)}, u32[]{:S(2)}) collective-permute-start(f32[4,32,3072]{2,1,0:T(8,128)S(1)} %get-tuple-element.368), channel_id=1, source_target_pairs={{0,6},{1,7},{2,0},{3,1},{4,2},{5,3},{6,4},{7,5},{8,14},{9,15},{10,... | collective-permute-start | bytes 4718600 | tf_op jit(solution)/shard_map/ppermute | solution.py:72
  271.0 67.6 %collective-permute-start.18 = (f32[4,32,3072]{2,1,0:T(8,128)S(1)}, f32[4,32,3072]{2,1,0:T(8,128)S(1)}, u32[]{:S(2)}, u32[]{:S(2)}) collective-permute-start(f32[4,32,3072]{2,1,0:T(8,128)S(1)} %get-tuple-element.369), channel_id=1, source_target_pairs={{0,2},{1,3},{2,4},{3,5},{4,6},{5,7},{6,0},{7,1},{8,10},{9,11},{10,... | collective-permute-start | bytes 4718600 | tf_op jit(solution)/shard_map/ppermute | solution.py:72
  289.1 62.8 %collective-permute-start.15 = (f32[4,32,3072]{2,1,0:T(8,128)S(1)}, f32[4,32,3072]{2,1,0:T(8,128)S(1)}, u32[]{:S(2)}, u32[]{:S(2)}) collective-permute-start(f32[4,32,3072]{2,1,0:T(8,128)S(1)} %get-tuple-element.370), channel_id=1, source_target_pairs={{0,6},{1,7},{2,0},{3,1},{4,2},{5,3},{6,4},{7,5},{8,14},{9,15},{10,... | collective-permute-start | bytes 4718600 | tf_op jit(solution)/shard_map/ppermute | solution.py:72
  291.8 60.2 %copy-start = (bf16[16,32,3072]{2,1,0:T(8,128)(2,1)S(1)}, bf16[16,32,3072]{2,1,0:T(8,128)(2,1)}, u32[]{:S(2)}) copy-start(bf16[16,32,3072]{2,1,0:T(8,128)(2,1)} %dres.3) | copy-start | bytes 9437188
  291.8 60.2 %copy-start.7 = (bf16[512,3072]{1,0:T(8,128)(2,1)S(1)}, bf16[512,3072]{1,0:T(8,128)(2,1)}, u32[]{:S(2)}) copy-start(bf16[512,3072]{1,0:T(8,128)(2,1)} %get-tuple-element.295) | copy-start | bytes 9437188
  291.8 60.2 %collective-permute-start.13 = (f32[4,32,3072]{2,1,0:T(8,128)S(1)}, f32[4,32,3072]{2,1,0:T(8,128)S(1)}, u32[]{:S(2)}, u32[]{:S(2)}) collective-permute-start(f32[4,32,3072]{2,1,0:T(8,128)S(1)} %get-tuple-element.371), channel_id=1, source_target_pairs={{0,2},{1,3},{2,4},{3,5},{4,6},{5,7},{6,0},{7,1},{8,10},{9,11},{10,... | collective-permute-start | bytes 4718600 | tf_op jit(solution)/shard_map/ppermute | solution.py:72
  373.6 60.1 %all-to-all-start.1 = ((bf16[8,96,3072]{2,1,0:T(8,128)(2,1)}), bf16[8,96,3072]{2,1,0:T(8,128)(2,1)}, u32[]{:S(2)}, u32[]{:S(2)}) async-start(bf16[8,96,3072]{2,1,0:T(8,128)(2,1)} %bitcast.77), calls=%async_computation.1 | async-start | bytes 9437184 | tf_op jit(solution)/shard_map/all_to_all | solution.py:277
  378.6 59.4 %copy-start.26 = (s32[768]{0:T(1024)S(1)}, s32[768]{0:T(1024)}, u32[]{:S(2)}) copy-start(s32[768]{0:T(1024)} %sub.174) | copy-start | bytes 9220
  434.5 19.4 %all-to-all-start.2 = ((f32[8,1,3072]{2,1,0:T(1,128)}), f32[8,1,3072]{2,1,0:T(1,128)S(1)}, u32[]{:S(2)}, u32[]{:S(2)}) async-start(f32[8,1,3072]{2,1,0:T(1,128)} %broadcast_in_dim.108), calls=%async_computation.2 | async-start | bytes 196608 | tf_op jit(solution)/shard_map/all_to_all | solution.py:288
  438.0 16.5 %copy-start.9 = (bf16[16,32,3072]{2,1,0:T(8,128)(2,1)S(1)}, bf16[16,32,3072]{2,1,0:T(8,128)(2,1)}, u32[]{:S(2)}) copy-start(bf16[16,32,3072]{2,1,0:T(8,128)(2,1)} %get-tuple-element.310) | copy-start | bytes 9437188
  438.1 16.5 %copy-start.14 = (s32[8,512]{1,0:T(8,128)S(1)}, s32[8,512]{1,0:T(8,128)}, u32[]{:S(2)}) copy-start(s32[8,512]{1,0:T(8,128)} %copy-done.12) | copy-start | bytes 49156
  438.1 16.5 %copy-start.16 = (s32[8,512]{1,0:T(8,128)S(1)}, s32[8,512]{1,0:T(8,128)}, u32[]{:S(2)}) copy-start(s32[8,512]{1,0:T(8,128)} %copy-done.15) | copy-start | bytes 49156
  438.1 16.5 %copy-start.18 = (s32[8,512]{1,0:T(8,128)S(1)}, s32[8,512]{1,0:T(8,128)}, u32[]{:S(2)}) copy-start(s32[8,512]{1,0:T(8,128)} %copy-done.17) | copy-start | bytes 49156
  438.1 16.5 %copy-start.20 = (s32[1,512]{1,0:T(1,128)S(1)}, s32[1,512]{1,0:T(1,128)}, u32[]{:S(2)}) copy-start(s32[1,512]{1,0:T(1,128)} %get-tuple-element.360) | copy-start | bytes 6148
  (8 other events, 66.6 us)
